TPU v7x, 32 devices: a whole 2x2x4 slice. The times are simulated.
32 devices in a mesh: blk: 4 (over y, x), grp: 8 (over z, core).
Axes of the slice: x: 2, y: 2, z: 4, core: 2. Of those that a mesh axis runs over, the one named last changes fastest.
Arguments:
- b3c: bfloat16 [384, 3, 32, 4096], P('blk', None, None, 'grp'), may hold values from -6 to 6
- green_occ: bfloat16 [384, 384], P('blk', 'grp'), may hold values from -0.3125 to 0.3125
- green_virt: bfloat16 [384, 384], P(None, 'grp'), may hold values from -0.625 to 0.625
- occ_mask: int32 [12, 12], replicated, may hold values from 0 to 1, as said below
- a_tiles: bfloat16 [128, 32, 1024], P(('blk', 'grp')), may hold values from -0.046875 to 0.046875
- tile_codes: int32 [128], P(('blk', 'grp')), may hold values from -1 to 143, as said below
Outputs:
- chi: float32 [512, 4096], P('blk', 'grp')
Inputs may be any that keep to these rules, and one draw needn't show every extreme that they name: `occ_mask`: the diagonal is 1. `tile_codes`: each device's 4 slots hold its live tiles first and -1 after them; some device has all 4 slots live; codes may repeat, and repeated tiles add.
All inputs are finite; a program needn't handle non-finite values.
Results may differ from a plain program's by a relative error of at most 0.0041.
Values may be sent and summed in bfloat16 or wider, within the bound.
No kernel may reach another device: no remote copies, remote signals or barrier semaphores. Data moves between devices by JAX's collectives and lax.ppermute only.
A program may use at most 192 MiB of HBM per device.

v0:
```python
import functools

import jax
import jax.numpy as jnp
from jax import lax
from jax.experimental import pallas as pl
from jax.experimental.pallas import tpu as pltpu
from jax.sharding import PartitionSpec as P


BS = 32
PB = 32
KB = 3
BAND = 3
PBD = 4
LANES = 128
NU_PART = 6
SUB = 2


def transform_kernel(pitch, begin, gv_ref, go_ref, b_ref, *refs):
    part, at_sub = pl.program_id(0) + begin, pl.program_id(1)
    halves = b_ref.shape[2] // LANES
    out_ref, scratch = refs[-1 - halves], refs[-halves:]
    rows = gv_ref.shape[1]
    lam = b_ref.shape[0]

    @pl.when(at_sub == 0)
    def _():
        for at in range(lam):
            r = jnp.dot(gv_ref[at // BS], b_ref[at], preferred_element_type=jnp.float32)
            for c, s in enumerate(scratch):
                s[pl.ds(at, rows, stride=pitch), :] = r[:, c * LANES : (c + 1) * LANES]

    for nb in range(SUB):
        here = at_sub * SUB + nb
        start = pl.multiple_of((part * (rows // BS) + here) * BS, BS)
        occ = go_ref[pl.ds(start, BAND * BS), :]
        zero = jnp.zeros_like(occ)
        occ = jnp.concatenate(
            [jnp.concatenate([occ, zero], axis=1), jnp.concatenate([zero, occ], axis=1)], axis=0
        )
        for i in range(BS // 2):
            at = (here * BS + 2 * i) * pitch
            w = jnp.concatenate(
                [
                    jnp.concatenate([s[pl.ds(at, lam), :], s[pl.ds(at + pitch, lam), :]], axis=0)
                    for s in scratch
                ],
                axis=1,
            )
            r = jnp.dot(occ, w.astype(jnp.bfloat16), preferred_element_type=jnp.float32)
            r = r.astype(jnp.bfloat16)
            for h in range(2):
                for j in range(BAND):
                    row = (h * BAND + j) * BS
                    to = (2 * i + h) * BS
                    out_ref[nb, BAND - 1 - j, to : to + BS, :] = r[row : row + BS]


def transform(b, gv, go, cols, which, begin, end, into=None):
    lam, band, _ = b.shape
    nb_total = gv.shape[1] // BS
    rows = NU_PART * BS
    pitch = lam + 2
    subs = NU_PART // SUB
    held = [] if into is None else [into]
    return pl.pallas_call(
        functools.partial(transform_kernel, pitch, begin),
        grid=(end - begin, subs),
        in_specs=[
            pl.BlockSpec((lam // BS, rows, band), lambda j, i: (0, j + begin, 0)),
            pl.BlockSpec(go.shape, lambda j, i: (0, 0)),
            pl.BlockSpec((lam, band, cols), lambda j, i: (0, 0, which)),
        ]
        + [pl.BlockSpec(memory_space=pl.ANY)] * len(held),
        out_specs=pl.BlockSpec(
            (SUB, BAND, BS * BS, cols), lambda j, i: ((j + begin) * subs + i, 0, 0, 0)
        ),
        out_shape=jax.ShapeDtypeStruct((nb_total, BAND, BS * BS, cols), jnp.bfloat16),
        scratch_shapes=[pltpu.VMEM((rows * pitch, LANES), jnp.float32)] * (cols // LANES),
        input_output_aliases={3: 0} if held else {},
        compiler_params=pltpu.CompilerParams(vmem_limit_bytes=62 * 2**20),
        cost_estimate=pl.CostEstimate(
            flops=75 * 10**8 * (end - begin), bytes_accessed=12 * 2**20, transcendentals=0
        ),
        name="transform",
    )(gv, go, b, *held)


def tiles_kernel(masks, halves, nu_ref, code_ref, *refs):
    groups, pairs = len(masks), KB * BAND
    sources, paired = refs[: 2 * groups], refs[2 * groups : 2 * groups + halves]
    out_ref, tiles, rhs, table, count, tile_sem, pair_sem = refs[-7:]
    aux = out_ref.shape[0] - 1
    slots = tiles.shape[2]
    cols = rhs.shape[3]

    def tile_copy(g, side):
        return pltpu.make_async_copy(sources[2 * g + side], tiles.at[g, side], tile_sem.at[g, side])

    def pair_copy(mask, at, p, h):
        return pltpu.make_async_copy(
            paired[h].at[nu_ref[mask * pairs + p], p % BAND], rhs.at[at, h], pair_sem.at[at, h]
        )

    for g, mask in enumerate(masks):
        for side in range(2):
            tile_copy(g, side).start()
        for p in range(pairs):
            for h in range(halves):
                pair_copy(mask, g * pairs + p, p, h).start()
    out_ref[...] = jnp.zeros_like(out_ref)
    for at in range(groups * pairs * 2):
        count[at] = 0
    for g, mask in enumerate(masks):
        for side in range(2):

            def put(s, carry):
                code = code_ref[(mask * 2 + side) * slots + s]

                @pl.when(code >= 0)
                def _():
                    at = (g * pairs + lax.rem(code, pairs)) * 2 + side
                    n = count[at]
                    table[at * slots + n] = lax.div(code, pairs) * 256 + s
                    count[at] = n + 1

                return carry

            lax.fori_loop(0, slots, put, 0)

    def item(g, pair, i):
        rows, lhs = [], []
        for side in range(2):
            for n in (2 * i, 2 * i + 1):
                at = pair * 2 + side
                entry = jnp.where(n < count[at], table[at * slots + n], aux * 256)
                rows.append(entry >> 8)
                lhs.append(tiles[g, side, entry & 255])
        lhs = jnp.concatenate(lhs, axis=0)
        for h in range(halves):
            r = jnp.dot(lhs, rhs[pair, h], preferred_element_type=jnp.float32)
            for t in range(4):
                out_ref[rows[t], :, h * cols : (h + 1) * cols] += r[t * PB : (t + 1) * PB]

    for g, mask in enumerate(masks):
        for side in range(2):
            tile_copy(g, side).wait()
        for p in range(pairs):
            for h in range(halves):
                pair_copy(mask, g * pairs + p, p, h).wait()
        for p in range(pairs):
            item(g, g * pairs + p, 0)

    def rest(pair, carry):
        more = (jnp.maximum(count[2 * pair], count[2 * pair + 1]) + 1) // 2

        def again(i, carry):
            item(pair // pairs, pair, i)
            return carry

        return lax.fori_loop(1, more, again, carry)

    lax.fori_loop(0, groups * pairs, rest, 0)


def contract(near, far, paired, nu, codes, aux, masks):
    halves = len(paired)
    cols = paired[0].shape[3]
    q = halves * cols
    groups, pairs = len(masks), KB * BAND
    slots = near[0].shape[0]
    acc = pl.BlockSpec((aux + 1, PB, q), lambda i, *_: (0, 0, 0))
    far_memory = pl.BlockSpec(memory_space=pltpu.HBM)
    return pl.pallas_call(
        functools.partial(tiles_kernel, masks, halves),
        grid_spec=pltpu.PrefetchScalarGridSpec(
            num_scalar_prefetch=2,
            grid=(1,),
            in_specs=[far_memory] * (2 * groups + halves),
            out_specs=acc,
            scratch_shapes=[
                pltpu.VMEM((groups, 2) + near[0].shape, jnp.bfloat16),
                pltpu.VMEM((groups * pairs, halves, BS * BS, cols), jnp.bfloat16),
                pltpu.SMEM((groups * pairs * 2 * slots,), jnp.int32),
                pltpu.SMEM((groups * pairs * 2,), jnp.int32),
                pltpu.SemaphoreType.DMA((groups, 2)),
                pltpu.SemaphoreType.DMA((groups * pairs, halves)),
            ],
        ),
        out_shape=jax.ShapeDtypeStruct((aux + 1, PB, q), jnp.float32),
        compiler_params=pltpu.CompilerParams(vmem_limit_bytes=62 * 2**20),
        cost_estimate=pl.CostEstimate(
            flops=40 * 10**8 * groups, bytes_accessed=12 * 2**20 * groups, transcendentals=0
        ),
        name="contract",
    )(
        nu,
        codes,
        *[side for pair in zip(near, far) for side in pair],
        *paired,
    )


def local(b3c, green_occ, green_virt, occ_mask, a_tiles, tile_codes):
    n_blk, n_grp = lax.axis_size("blk"), lax.axis_size("grp")
    group, member = lax.axis_index("blk"), lax.axis_index("grp")
    lam, _, _, q = b3c.shape
    basis, wide = green_virt.shape
    blocks = basis // BS
    aux = n_blk * PBD
    slots_here = a_tiles.shape[0]
    spread = n_grp // 2

    def grp_swap(a, bits):
        return lax.ppermute(a, "grp", [(i, i ^ bits) for i in range(n_grp)])

    def blk_swap(a, bits):
        return lax.ppermute(a, "blk", [(i, i ^ bits) for i in range(n_blk)])

    turned = a_tiles.reshape(slots_here, PB, BS, BS).swapaxes(2, 3).reshape(a_tiles.shape)

    coded = jnp.stack([tile_codes // (KB * BAND), tile_codes % (KB * BAND)])
    coded = jnp.where(tile_codes >= 0, coded, -1).astype(jnp.bfloat16)
    coded = jnp.pad(coded, ((0, 14), (0, wide - slots_here)))
    small = jnp.concatenate([green_virt, green_occ, coded], axis=0)[None]
    bit = 2
    while bit < n_grp:
        moved = grp_swap(small, bit)
        small = jnp.concatenate([small, moved], axis=0)
        bit *= 2
    small = jnp.concatenate([small, grp_swap(small, 1)], axis=0)
    relative = jnp.arange(n_grp, dtype=jnp.int32) ^ member
    order = relative % 2 * spread + relative // 2
    ordered = jnp.take(small[:, : basis + lam], order, axis=0)
    virt_all = ordered[:, :basis].swapaxes(0, 1).reshape(basis, basis)
    occ_rows = ordered[:, basis:].swapaxes(0, 1).reshape(lam, basis)
    code_rows = -(-2 * n_grp * slots_here // (16 * lam)) * 16
    part = small[:, basis + lam : basis + lam + 2, :slots_here].swapaxes(0, 1).reshape(2, -1)
    part = jnp.pad(part, ((0, 0), (0, code_rows // 2 * lam - part.shape[1])))
    part = part.reshape(code_rows, lam)
    received = []
    for mask in range(n_blk):
        mine = lax.dynamic_slice_in_dim(occ_rows, (group ^ mask) * lam, lam, 1)
        packet = jnp.concatenate([mine, part], axis=0)
        received.append(blk_swap(packet, mask) if mask else packet)
    received = jnp.stack(received)
    occ = jnp.take(received[:, :lam], jnp.arange(n_blk, dtype=jnp.int32) ^ group, axis=0)
    occ = occ.reshape(basis, lam)
    part = received[:, lam:].reshape(n_blk, 2, -1)[:, :, : n_grp * slots_here].astype(jnp.int32)
    codes = jnp.where(part[:, 0] >= 0, part[:, 0] * (KB * BAND) + part[:, 1], -1)
    codes = codes.reshape(-1)

    mask = lax.dynamic_slice_in_dim(occ_mask, group * KB, KB, 1)
    mask = jnp.repeat(jnp.repeat(mask, BS, axis=0), BS, axis=1).astype(jnp.bfloat16)
    occ = occ * mask
    occ = jnp.concatenate([occ[-(BAND - 1) * BS :], occ], axis=0)
    virt = jnp.concatenate([virt_all, virt_all[:, : (BAND - 1) * BS]], axis=1)
    virt = lax.dynamic_slice_in_dim(virt, group * lam, lam + (BAND - 1) * BS, 1)
    virt = jnp.stack([virt[:, l * BS : (l + BAND) * BS] for l in range(KB)])

    owners = jnp.arange(n_blk, dtype=jnp.int32) ^ group
    pair = jnp.arange(KB * BAND, dtype=jnp.int32)
    nu = ((owners[:, None] * KB + (pair // BAND + pair % BAND)[None, :]) % blocks).reshape(-1)

    b = b3c.reshape(lam, BAND * BS, q)
    cols = min(2 * LANES, q)
    parts = blocks // NU_PART
    hops = []
    for d in range(1, spread):
        hops.append(grp_swap(turned, 2 * d))
    paired = transform(b, virt, occ, cols, 0, 0, 1)
    hops, paired = lax.optimization_barrier((hops, paired))
    near = {0: jnp.concatenate([turned] + hops)}
    bits = [1 << i for i in range((n_blk - 1).bit_length())]
    for to in bits:
        near[to] = blk_swap(near[0], to)
    far = {0: grp_swap(near[0], 1)}
    paired = [transform(b, virt, occ, cols, 0, 1, parts, paired)]
    paired += [transform(b, virt, occ, cols, h, 0, parts) for h in range(1, q // cols)]
    arriving, paired = lax.optimization_barrier(([[near[to]] for to in bits], paired))
    levels = [[m for m in range(n_blk) if m.bit_count() == n] for n in range(1, len(bits) + 1)]
    half = near[0].shape[0] // 2
    sums, first = [], [0]
    for masks, after in zip(levels, levels[1:] + [[]]):
        for to, pieces in zip(masks, arriving):
            near[to] = pieces[0] if len(pieces) == 1 else jnp.concatenate(pieces)
        arriving = []
        for to in after:
            low, high = to & -to, 1 << (to.bit_length() - 1)
            arriving.append(
                [blk_swap(near[to ^ low][:half], low), blk_swap(near[to ^ high][half:], high)]
            )
        for to in masks:
            far[to] = grp_swap(near[to], 1)
        now = tuple(first + masks)
        first = []
        chi = contract([near[m] for m in now], [far[m] for m in now], paired, nu, codes, aux, now)
        arriving, chi = lax.optimization_barrier((arriving, chi))
        sums.append(chi[:aux].reshape(n_blk, PBD * PB, q))

    def piece(d):
        return sum(lax.dynamic_index_in_dim(chi, group ^ d, 0, False) for chi in sums)

    total = piece(0)
    for d in range(1, n_blk):
        total = total + blk_swap(piece(d).astype(jnp.bfloat16), d).astype(jnp.float32)
    return total


def solution(mesh):
    in_specs = (
        P("blk", None, None, "grp"),
        P("blk", "grp"),
        P(None, "grp"),
        P(),
        P(("blk", "grp"), None, None),
        P(("blk", "grp")),
    )
    out_specs = P("blk", "grp")
    return jax.shard_map(local, mesh=mesh, in_specs=in_specs, out_specs=out_specs, check_vma=False)
```

profile of v0, /device:TPU:0, one launch (start us, length us, event | category | flops | bytes accessed | tf_op | source)
XLA Modules:
  0.0 130.7 jit_solution(12427912344567389296)
XLA Ops:
  0.0 1.8 %reshape.194 = bf16[4,32,32,32]{3,2,1,0:T(8,128)(2,1)S(1)} reshape(bf16[4,32,1024]{2,1,0:T(8,128)(2,1)} %param.10) | data formatting | bytes 524288 | tf_op jit(solution)/shard_map/reshape | solution.py:222
  2.5 1.1 reshape.195
  3.6 3.1 %collective-permute-start = (bf16[4,32,1024]{2,1,0:T(8,128)(2,1)S(1)}, bf16[4,32,1024]{2,1,0:T(8,128)(2,1)S(1)}, u32[]{:S(2)}, u32[]{:S(2)}) collective-permute-start(bf16[4,32,1024]{2,1,0:T(8,128)(2,1)S(1)} %reshape.195), channel_id=1, source_target_pairs={{0,2},{1,3},{2,0},{3,1},{4,6},{5,7},{6,4},{7,5},{8,10},{9,11},{10,... | collective-permute-start | bytes 786440 | tf_op jit(solution)/shard_map/ppermute | solution.py:217
  6.8 2.6 %collective-permute-start.1 = (bf16[4,32,1024]{2,1,0:T(8,128)(2,1)S(1)}, bf16[4,32,1024]{2,1,0:T(8,128)(2,1)S(1)}, u32[]{:S(2)}, u32[]{:S(2)}) collective-permute-start(bf16[4,32,1024]{2,1,0:T(8,128)(2,1)S(1)} %reshape.195), channel_id=1, source_target_pairs={{0,4},{1,5},{2,6},{3,7},{4,0},{5,1},{6,2},{7,3},{8,12},{9,13},{10,... | collective-permute-start | bytes 786440 | tf_op jit(solution)/shard_map/ppermute | solution.py:217
  10.8 0.9 fusion.9
  12.8 6.8 %collective-permute-done.3 = bf16[1,496,48]{1,2,0:T(8,128)(2,1)S(1)} collective-permute-done((bf16[1,496,48]{1,2,0:T(8,128)(2,1)S(1)}, bf16[1,496,48]{1,2,0:T(8,128)(2,1)S(1)}, u32[]{:S(2)}, u32[]{:S(2)}) %collective-permute-start.3) | collective-permute-done | bytes 47648 | tf_op jit(solution)/shard_map/ppermute | solution.py:217
  19.6 3.0 %collective-permute-start.4 = (bf16[2,496,48]{1,2,0:T(8,128)(2,1)S(1)}, bf16[2,496,48]{1,2,0:T(8,128)(2,1)S(1)}, u32[]{:S(2)}, u32[]{:S(2)}) collective-permute-start(bf16[2,496,48]{1,2,0:T(8,128)(2,1)S(1)} %pad_maximum_fusion.5), channel_id=1, source_target_pairs={{0,4},{1,5},{2,6},{3,7},{4,0},{5,1},{6,2},{7,3},{8,12},{9,13},{10,... | collective-permute-start | bytes 285704 | tf_op jit(solution)/shard_map/ppermute | solution.py:217
  22.6 4.0 %collective-permute-done.4 = bf16[2,496,48]{1,2,0:T(8,128)(2,1)S(1)} collective-permute-done((bf16[2,496,48]{1,2,0:T(8,128)(2,1)S(1)}, bf16[2,496,48]{1,2,0:T(8,128)(2,1)S(1)}, u32[]{:S(2)}, u32[]{:S(2)}) %collective-permute-start.4) | collective-permute-done | bytes 95264 | tf_op jit(solution)/shard_map/ppermute | solution.py:217
  29.8 1.6 %collective-permute-start.6 = (bf16[112,96]{1,0:T(8,128)(2,1)S(1)}, bf16[112,96]{1,0:T(8,128)(2,1)S(1)}, u32[]{:S(2)}, u32[]{:S(2)}) collective-permute-start(bf16[112,96]{1,0:T(8,128)(2,1)S(1)} %get-tuple-element.38), channel_id=1, source_target_pairs={{0,8},{8,0},{16,24},{24,16},{1,9},{9,1},{17,25},{25,17},{2,10},{10... | collective-permute-start | bytes 64520 | tf_op jit(solution)/shard_map/ppermute | solution.py:220
  31.4 1.5 %collective-permute-start.7 = (bf16[112,96]{1,0:T(8,128)(2,1)S(1)}, bf16[112,96]{1,0:T(8,128)(2,1)S(1)}, u32[]{:S(2)}, u32[]{:S(2)}) collective-permute-start(bf16[112,96]{1,0:T(8,128)(2,1)S(1)} %get-tuple-element.39), channel_id=1, source_target_pairs={{0,16},{8,24},{16,0},{24,8},{1,17},{9,25},{17,1},{25,9},{2,18},{10... | collective-permute-start | bytes 64520 | tf_op jit(solution)/shard_map/ppermute | solution.py:220
  34.0 0.8 pad_maximum_fusion.1.gv_ref
  34.7 2.7 %collective-permute-start.2 = (bf16[4,32,1024]{2,1,0:T(8,128)(2,1)S(1)}, bf16[4,32,1024]{2,1,0:T(8,128)(2,1)S(1)}, u32[]{:S(2)}, u32[]{:S(2)}) collective-permute-start(bf16[4,32,1024]{2,1,0:T(8,128)(2,1)S(1)} %reshape.195), channel_id=1, source_target_pairs={{0,6},{1,7},{2,4},{3,5},{4,2},{5,3},{6,0},{7,1},{8,14},{9,15},{10,... | collective-permute-start | bytes 786440 | tf_op jit(solution)/shard_map/ppermute | solution.py:217
  39.1 10.5 %transform.3.refs_0_ = bf16[12,3,1024,256]{3,2,1,0:T(8,128)(2,1)} custom-call(bf16[3,384,96]{2,1,0:T(8,128)(2,1)} %pad_maximum_fusion.1.gv_ref, bf16[448,96]{1,0:T(8,128)(2,1)} %pad_maximum_fusion.4.go_ref, bf16[96,96,512]{2,1,0:T(8,128)(2,1)} %bitcast.56), custom_call_target="tpu_custom_call" | custom-call | flops 7500000256 | bytes 12582912 | tf_op jit(solution)/shard_map/transform/pallas_call | solution.py:68
  49.6 0.7 constant_dynamic-update-slice_fusion.2
  51.7 1.3 collective-permute-start.10
  53.0 1.5 %collective-permute-start.9 = (bf16[16,32,1024]{2,1,0:T(8,128)(2,1)}, bf16[16,32,1024]{2,1,0:T(8,128)(2,1)}, u32[]{:S(2)}, u32[]{:S(2)}) collective-permute-start(bf16[16,32,1024]{2,1,0:T(8,128)(2,1)} %constant_dynamic-update-slice_fusion.refs_0_), channel_id=1, source_target_pairs={{0,8},{8,0},{16,24},{24,16},{1,9},{9,1},{17,25},{25,17},{2,10},{10... | collective-permute-start | bytes 3145736 | tf_op jit(solution)/shard_map/ppermute | solution.py:220
  54.5 16.6 %transform.5.refs_7_.refs_3_ = bf16[12,3,1024,256]{3,2,1,0:T(8,128)(2,1)} custom-call(bf16[3,384,96]{2,1,0:T(8,128)(2,1)} %pad_maximum_fusion.1.gv_ref, bf16[448,96]{1,0:T(8,128)(2,1)} %pad_maximum_fusion.4.go_ref, bf16[96,96,512]{2,1,0:T(8,128)(2,1)} %bitcast.57), custom_call_target="tpu_custom_call" | custom-call | flops 15000000512 | bytes 12582912 | tf_op jit(solution)/shard_map/transform/pallas_call | solution.py:68
  71.2 10.7 %transform.4.refs_6_.refs_2_ = bf16[12,3,1024,256]{3,2,1,0:T(8,128)(2,1)} custom-call(bf16[3,384,96]{2,1,0:T(8,128)(2,1)} %pad_maximum_fusion.1.gv_ref, bf16[448,96]{1,0:T(8,128)(2,1)} %pad_maximum_fusion.4.go_ref, bf16[96,96,512]{2,1,0:T(8,128)(2,1)} %bitcast.58, bf16[12,3,1024,256]{3,2,1,0:T(8,128)(2,1)} %transform.3.refs_0_), custom_call_target="tpu_custom_call", output_to_operand_aliasing={{}: (3, {})} | custom-call | flops 7500000256 | bytes 12582912 | tf_op jit(solution)/shard_map/transform/pallas_call | solution.py:68
  84.0 0.8 slice.65
  84.8 1.9 %slice.66 = bf16[8,32,1024]{2,1,0:T(8,128)(2,1)} slice(bf16[16,32,1024]{2,1,0:T(8,128)(2,1)} %collective-permute-done.9.refs_2_), slice={[8:16], [0:32], [0:1024]} | slice | bytes 1048576 | tf_op jit(solution)/shard_map/slice | solution.py:293
  87.2 0.7 collective-permute-start.12
  87.9 18.0 %contract.2 = f32[17,32,512]{2,1,0:T(8,128)} custom-call(s32[36]{0:T(128)} %and_select_fusion.nu_ref, s32[128]{0:T(128)} %select_n.180.code_ref, bf16[16,32,1024]{2,1,0:T(8,128)(2,1)} %constant_dynamic-update-slice_fusion.refs_0_, bf16[16,32,1024]{2,1,0:T(8,128)(2,1)} %collective-permute-done.13.refs_1_, ...), custom_call_target="tpu_custom_call" | custom-call | flops 12000000000 | bytes 37748736 | tf_op jit(solution)/shard_map/contract/pallas_call | solution.py:176
  106.0 1.1 constant_dynamic-update-slice_fusion.4.refs_0_
  107.2 0.9 copy-done.3
  108.1 1.3 %slice.71 = f32[16,32,512]{2,1,0:T(8,128)S(1)} slice(f32[17,32,512]{2,1,0:T(8,128)} %contract.2), slice={[0:16], [0:32], [0:512]} | slice | bytes 2097152 | tf_op jit(solution)/shard_map/slice | solution.py:301
  110.0 8.9 %contract.3 = f32[17,32,512]{2,1,0:T(8,128)} custom-call(s32[36]{0:T(128)} %and_select_fusion.nu_ref, s32[128]{0:T(128)} %select_n.180.code_ref, bf16[16,32,1024]{2,1,0:T(8,128)(2,1)} %copy-done.3, bf16[16,32,1024]{2,1,0:T(8,128)(2,1)} %collective-permute-done.16.refs_1_, bf16[12,3,1024,256]{3,2,1,0:T(8,128)(2,1)} %transform.4.refs_6_.refs_2_, ...), custom_call_target="tpu_custom_call" | custom-call | flops 4000000000 | bytes 12582912 | tf_op jit(solution)/shard_map/contract/pallas_call | solution.py:176
  118.9 1.3 %slice.89 = f32[16,32,512]{2,1,0:T(8,128)S(1)} slice(f32[17,32,512]{2,1,0:T(8,128)} %contract.3), slice={[0:16], [0:32], [0:512]} | slice | bytes 2097152 | tf_op jit(solution)/shard_map/slice | solution.py:301
  120.3 1.5 %collective-permute-start.17 = (bf16[128,512]{1,0:T(8,128)(2,1)S(1)}, bf16[128,512]{1,0:T(8,128)(2,1)S(1)}, u32[]{:S(2)}, u32[]{:S(2)}) collective-permute-start(bf16[128,512]{1,0:T(8,128)(2,1)S(1)} %get-tuple-element.27), channel_id=1, source_target_pairs={{0,8},{8,0},{16,24},{24,16},{1,9},{9,1},{17,25},{25,17},{2,10},{10... | collective-permute-start | bytes 393224 | tf_op jit(solution)/shard_map/ppermute | solution.py:220
  121.8 1.4 %collective-permute-start.18 = (bf16[128,512]{1,0:T(8,128)(2,1)S(1)}, bf16[128,512]{1,0:T(8,128)(2,1)S(1)}, u32[]{:S(2)}, u32[]{:S(2)}) collective-permute-start(bf16[128,512]{1,0:T(8,128)(2,1)S(1)} %get-tuple-element.29), channel_id=1, source_target_pairs={{0,16},{8,24},{16,0},{24,8},{1,17},{9,25},{17,1},{25,9},{2,18},{10... | collective-permute-start | bytes 393224 | tf_op jit(solution)/shard_map/ppermute | solution.py:220
  123.9 2.5 %collective-permute-done.17 = bf16[128,512]{1,0:T(8,128)(2,1)S(1)} collective-permute-done((bf16[128,512]{1,0:T(8,128)(2,1)S(1)}, bf16[128,512]{1,0:T(8,128)(2,1)S(1)}, u32[]{:S(2)}, u32[]{:S(2)}) %collective-permute-start.17) | collective-permute-done | bytes 131104 | tf_op jit(solution)/shard_map/ppermute | solution.py:220
  126.4 3.6 %collective-permute-done.18 = bf16[128,512]{1,0:T(8,128)(2,1)S(1)} collective-permute-done((bf16[128,512]{1,0:T(8,128)(2,1)S(1)}, bf16[128,512]{1,0:T(8,128)(2,1)S(1)}, u32[]{:S(2)}, u32[]{:S(2)}) %collective-permute-start.18) | collective-permute-done | bytes 131104 | tf_op jit(solution)/shard_map/ppermute | solution.py:220
  129.9 0.8 fusion.1
  (93 shorter events, 14.4 us)
Async XLA Ops:
  0.0 12.2 %copy-start = (s32[12,12]{1,0:T(8,128)S(1)}, s32[12,12]{1,0:T(8,128)}, u32[]{:S(2)}) copy-start(s32[12,12]{1,0:T(8,128)} %param.9) | copy-start | bytes 1732
  3.6 45.9 %collective-permute-start = (bf16[4,32,1024]{2,1,0:T(8,128)(2,1)S(1)}, bf16[4,32,1024]{2,1,0:T(8,128)(2,1)S(1)}, u32[]{:S(2)}, u32[]{:S(2)}) collective-permute-start(bf16[4,32,1024]{2,1,0:T(8,128)(2,1)S(1)} %reshape.195), channel_id=1, source_target_pairs={{0,2},{1,3},{2,0},{3,1},{4,6},{5,7},{6,4},{7,5},{8,10},{9,11},{10,... | collective-permute-start | bytes 786440 | tf_op jit(solution)/shard_map/ppermute | solution.py:217
  6.8 42.8 %collective-permute-start.1 = (bf16[4,32,1024]{2,1,0:T(8,128)(2,1)S(1)}, bf16[4,32,1024]{2,1,0:T(8,128)(2,1)S(1)}, u32[]{:S(2)}, u32[]{:S(2)}) collective-permute-start(bf16[4,32,1024]{2,1,0:T(8,128)(2,1)S(1)} %reshape.195), channel_id=1, source_target_pairs={{0,4},{1,5},{2,6},{3,7},{4,0},{5,1},{6,2},{7,3},{8,12},{9,13},{10,... | collective-permute-start | bytes 786440 | tf_op jit(solution)/shard_map/ppermute | solution.py:217
  11.7 8.0 %collective-permute-start.3 = (bf16[1,496,48]{1,2,0:T(8,128)(2,1)S(1)}, bf16[1,496,48]{1,2,0:T(8,128)(2,1)S(1)}, u32[]{:S(2)}, u32[]{:S(2)}) collective-permute-start(bf16[1,496,48]{1,2,0:T(8,128)(2,1)S(1)} %fusion.9), channel_id=1, source_target_pairs={{0,2},{1,3},{2,0},{3,1},{4,6},{5,7},{6,4},{7,5},{8,10},{9,11},{10,... | collective-permute-start | bytes 142856 | tf_op jit(solution)/shard_map/ppermute | solution.py:217
  19.6 7.0 %collective-permute-start.4 = (bf16[2,496,48]{1,2,0:T(8,128)(2,1)S(1)}, bf16[2,496,48]{1,2,0:T(8,128)(2,1)S(1)}, u32[]{:S(2)}, u32[]{:S(2)}) collective-permute-start(bf16[2,496,48]{1,2,0:T(8,128)(2,1)S(1)} %pad_maximum_fusion.5), channel_id=1, source_target_pairs={{0,4},{1,5},{2,6},{3,7},{4,0},{5,1},{6,2},{7,3},{8,12},{9,13},{10,... | collective-permute-start | bytes 285704 | tf_op jit(solution)/shard_map/ppermute | solution.py:217
  26.7 1.5 %collective-permute-start.5 = (bf16[4,496,48]{1,2,0:T(8,128)(2,1)S(1)}, bf16[4,496,48]{1,2,0:T(8,128)(2,1)S(1)}, u32[]{:S(2)}, u32[]{:S(2)}) collective-permute-start(bf16[4,496,48]{1,2,0:T(8,128)(2,1)S(1)} %pad_maximum_fusion.2), channel_id=1, source_target_pairs={{0,1},{1,0},{2,3},{3,2},{4,5},{5,4},{6,7},{7,6},{8,9},{9,8},{10,11... | collective-permute-start | bytes 571400 | tf_op jit(solution)/shard_map/ppermute | solution.py:217
  29.8 4.9 %collective-permute-start.6 = (bf16[112,96]{1,0:T(8,128)(2,1)S(1)}, bf16[112,96]{1,0:T(8,128)(2,1)S(1)}, u32[]{:S(2)}, u32[]{:S(2)}) collective-permute-start(bf16[112,96]{1,0:T(8,128)(2,1)S(1)} %get-tuple-element.38), channel_id=1, source_target_pairs={{0,8},{8,0},{16,24},{24,16},{1,9},{9,1},{17,25},{25,17},{2,10},{10... | collective-permute-start | bytes 64520 | tf_op jit(solution)/shard_map/ppermute | solution.py:220
  31.4 6.1 %collective-permute-start.7 = (bf16[112,96]{1,0:T(8,128)(2,1)S(1)}, bf16[112,96]{1,0:T(8,128)(2,1)S(1)}, u32[]{:S(2)}, u32[]{:S(2)}) collective-permute-start(bf16[112,96]{1,0:T(8,128)(2,1)S(1)} %get-tuple-element.39), channel_id=1, source_target_pairs={{0,16},{8,24},{16,0},{24,8},{1,17},{9,25},{17,1},{25,9},{2,18},{10... | collective-permute-start | bytes 64520 | tf_op jit(solution)/shard_map/ppermute | solution.py:220
  32.9 4.8 %collective-permute-start.8 = (bf16[112,96]{1,0:T(8,128)(2,1)S(1)}, bf16[112,96]{1,0:T(8,128)(2,1)S(1)}, u32[]{:S(2)}, u32[]{:S(2)}) collective-permute-start(bf16[112,96]{1,0:T(8,128)(2,1)S(1)} %get-tuple-element.40), channel_id=1, source_target_pairs={{0,24},{8,16},{16,8},{24,0},{1,25},{9,17},{17,9},{25,1},{2,26},{10... | collective-permute-start | bytes 64520 | tf_op jit(solution)/shard_map/ppermute | solution.py:220
  34.7 14.9 %collective-permute-start.2 = (bf16[4,32,1024]{2,1,0:T(8,128)(2,1)S(1)}, bf16[4,32,1024]{2,1,0:T(8,128)(2,1)S(1)}, u32[]{:S(2)}, u32[]{:S(2)}) collective-permute-start(bf16[4,32,1024]{2,1,0:T(8,128)(2,1)S(1)} %reshape.195), channel_id=1, source_target_pairs={{0,6},{1,7},{2,4},{3,5},{4,2},{5,3},{6,0},{7,1},{8,14},{9,15},{10,... | collective-permute-start | bytes 786440 | tf_op jit(solution)/shard_map/ppermute | solution.py:217
  51.7 30.1 %collective-permute-start.10 = (bf16[16,32,1024]{2,1,0:T(8,128)(2,1)}, bf16[16,32,1024]{2,1,0:T(8,128)(2,1)S(1)}, u32[]{:S(2)}, u32[]{:S(2)}) collective-permute-start(bf16[16,32,1024]{2,1,0:T(8,128)(2,1)} %constant_dynamic-update-slice_fusion.refs_0_), channel_id=1, source_target_pairs={{0,16},{8,24},{16,0},{24,8},{1,17},{9,25},{17,1},{25,9},{2,18},{10... | collective-permute-start | bytes 3145736 | tf_op jit(solution)/shard_map/ppermute | solution.py:220
  53.0 28.8 %collective-permute-start.9 = (bf16[16,32,1024]{2,1,0:T(8,128)(2,1)}, bf16[16,32,1024]{2,1,0:T(8,128)(2,1)}, u32[]{:S(2)}, u32[]{:S(2)}) collective-permute-start(bf16[16,32,1024]{2,1,0:T(8,128)(2,1)} %constant_dynamic-update-slice_fusion.refs_0_), channel_id=1, source_target_pairs={{0,8},{8,0},{16,24},{24,16},{1,9},{9,1},{17,25},{25,17},{2,10},{10... | collective-permute-start | bytes 3145736 | tf_op jit(solution)/shard_map/ppermute | solution.py:220
  71.2 16.8 %collective-permute-start.13 = (bf16[16,32,1024]{2,1,0:T(8,128)(2,1)}, bf16[16,32,1024]{2,1,0:T(8,128)(2,1)}, u32[]{:S(2)}, u32[]{:S(2)}) collective-permute-start(bf16[16,32,1024]{2,1,0:T(8,128)(2,1)} %constant_dynamic-update-slice_fusion.refs_0_), channel_id=1, source_target_pairs={{0,1},{1,0},{2,3},{3,2},{4,5},{5,4},{6,7},{7,6},{8,9},{9,8},{10,11... | collective-permute-start | bytes 3145736 | tf_op jit(solution)/shard_map/ppermute | solution.py:217
  81.9 6.1 %copy-start.2 = (bf16[16,32,1024]{2,1,0:T(8,128)(2,1)}, bf16[16,32,1024]{2,1,0:T(8,128)(2,1)S(1)}, u32[]{:S(2)}) copy-start(bf16[16,32,1024]{2,1,0:T(8,128)(2,1)S(1)} %collective-permute-done.10.refs_4_) | copy-start | bytes 3145732
  81.9 6.0 %collective-permute-start.14 = (bf16[16,32,1024]{2,1,0:T(8,128)(2,1)}, bf16[16,32,1024]{2,1,0:T(8,128)(2,1)}, u32[]{:S(2)}, u32[]{:S(2)}) collective-permute-start(bf16[16,32,1024]{2,1,0:T(8,128)(2,1)} %collective-permute-done.9.refs_2_), channel_id=1, source_target_pairs={{0,1},{1,0},{2,3},{3,2},{4,5},{5,4},{6,7},{7,6},{8,9},{9,8},{10,11... | collective-permute-start | bytes 3145736 | tf_op jit(solution)/shard_map/ppermute | solution.py:217
  82.2 5.7 %collective-permute-start.15 = (bf16[16,32,1024]{2,1,0:T(8,128)(2,1)S(1)}, bf16[16,32,1024]{2,1,0:T(8,128)(2,1)}, u32[]{:S(2)}, u32[]{:S(2)}) collective-permute-start(bf16[16,32,1024]{2,1,0:T(8,128)(2,1)S(1)} %collective-permute-done.10.refs_4_), channel_id=1, source_target_pairs={{0,1},{1,0},{2,3},{3,2},{4,5},{5,4},{6,7},{7,6},{8,9},{9,8},{10,11... | collective-permute-start | bytes 3145736 | tf_op jit(solution)/shard_map/ppermute | solution.py:217
  86.6 19.3 %collective-permute-start.11 = (bf16[8,32,1024]{2,1,0:T(8,128)(2,1)}, bf16[8,32,1024]{2,1,0:T(8,128)(2,1)S(1)}, u32[]{:S(2)}, u32[]{:S(2)}) collective-permute-start(bf16[8,32,1024]{2,1,0:T(8,128)(2,1)} %slice.65), channel_id=1, source_target_pairs={{0,8},{8,0},{16,24},{24,16},{1,9},{9,1},{17,25},{25,17},{2,10},{10... | collective-permute-start | bytes 1572872 | tf_op jit(solution)/shard_map/ppermute | solution.py:220
  87.2 18.8 %collective-permute-start.12 = (bf16[8,32,1024]{2,1,0:T(8,128)(2,1)}, bf16[8,32,1024]{2,1,0:T(8,128)(2,1)}, u32[]{:S(2)}, u32[]{:S(2)}) collective-permute-start(bf16[8,32,1024]{2,1,0:T(8,128)(2,1)} %slice.66), channel_id=1, source_target_pairs={{0,16},{8,24},{16,0},{24,8},{1,17},{9,25},{17,1},{25,9},{2,18},{10... | collective-permute-start | bytes 1572872 | tf_op jit(solution)/shard_map/ppermute | solution.py:220
  107.1 1.0 copy-start.3
  107.1 2.9 %collective-permute-start.16 = (bf16[16,32,1024]{2,1,0:T(8,128)(2,1)S(1)}, bf16[16,32,1024]{2,1,0:T(8,128)(2,1)}, u32[]{:S(2)}, u32[]{:S(2)}) collective-permute-start(bf16[16,32,1024]{2,1,0:T(8,128)(2,1)S(1)} %constant_dynamic-update-slice_fusion.4.refs_0_), channel_id=1, source_target_pairs={{0,1},{1,0},{2,3},{3,2},{4,5},{5,4},{6,7},{7,6},{8,9},{9,8},{10,11... | collective-permute-start | bytes 3145736 | tf_op jit(solution)/shard_map/ppermute | solution.py:217
  108.1 22.6 %copy-start.1 = (s32[12,12]{1,0:T(8,128)S(1)}, s32[12,12]{1,0:T(8,128)}, u32[]{:S(2)}) copy-start(s32[12,12]{1,0:T(8,128)} %param.9) | copy-start | bytes 1732
  120.3 6.0 %collective-permute-start.17 = (bf16[128,512]{1,0:T(8,128)(2,1)S(1)}, bf16[128,512]{1,0:T(8,128)(2,1)S(1)}, u32[]{:S(2)}, u32[]{:S(2)}) collective-permute-start(bf16[128,512]{1,0:T(8,128)(2,1)S(1)} %get-tuple-element.27), channel_id=1, source_target_pairs={{0,8},{8,0},{16,24},{24,16},{1,9},{9,1},{17,25},{25,17},{2,10},{10... | collective-permute-start | bytes 393224 | tf_op jit(solution)/shard_map/ppermute | solution.py:220
  121.8 8.1 %collective-permute-start.18 = (bf16[128,512]{1,0:T(8,128)(2,1)S(1)}, bf16[128,512]{1,0:T(8,128)(2,1)S(1)}, u32[]{:S(2)}, u32[]{:S(2)}) collective-permute-start(bf16[128,512]{1,0:T(8,128)(2,1)S(1)} %get-tuple-element.29), channel_id=1, source_target_pairs={{0,16},{8,24},{16,0},{24,8},{1,17},{9,25},{17,1},{25,9},{2,18},{10... | collective-permute-start | bytes 393224 | tf_op jit(solution)/shard_map/ppermute | solution.py:220
  123.2 6.7 %collective-permute-start.19 = (bf16[128,512]{1,0:T(8,128)(2,1)S(1)}, bf16[128,512]{1,0:T(8,128)(2,1)S(1)}, u32[]{:S(2)}, u32[]{:S(2)}) collective-permute-start(bf16[128,512]{1,0:T(8,128)(2,1)S(1)} %get-tuple-element.28), channel_id=1, source_target_pairs={{0,24},{8,16},{16,8},{24,0},{1,25},{9,17},{17,9},{25,1},{2,26},{10... | collective-permute-start | bytes 393224 | tf_op jit(solution)/shard_map/ppermute | solution.py:220
where the time goes:
time: 131 us
  Pallas kernels  64.7 us (49%)
  starting transfers between devices  23.7 us (18%)
  waiting for transfers between devices  18.4 us (14%)
  local copies, waits for them, and re-layouts  17.6 us (13%)
  other arithmetic  5.94 us (5%)
    pallas_call x3, Pallas kernels, transform(): pl.pallas_call(functools.partial(transform_kernel, pitch, begin), grid=(e...  37.8 us
    pallas_call x2, Pallas kernels, contract(): pl.pallas_call(functools.partial(tiles_kernel, masks, halves), grid_spec=...  26.9 us
    ppermute x10, starting transfers between devices, grp_swap(): return lax.ppermute(a, 'grp', [(i, i ^ bits) for i in range(n_grp)])  12.6 us
    ppermute x10, waiting for transfers between devices, grp_swap(): return lax.ppermute(a, 'grp', [(i, i ^ bits) for i in range(n_grp)])  12.1 us
    ppermute x10, starting transfers between devices, blk_swap(): return lax.ppermute(a, 'blk', [(i, i ^ bits) for i in range(n_blk)])  11.2 us
    ppermute x10, waiting for transfers between devices, blk_swap(): return lax.ppermute(a, 'blk', [(i, i ^ bits) for i in range(n_blk)])  6.27 us
    unnamed x18, local copies, waits for them, and re-layouts  3.72 us
    reshape x3, local copies, waits for them, and re-layouts, local(): a_tiles.reshape(slots_here, PB, BS, BS).swapaxes(2, 3)  3.62 us
  transfers between devices with their start and end apart: 20, of which 7 were waited for; matrix products, arithmetic and copies ran while one was open for 10% of the time, Pallas kernels for 43%

commit v1 on v0

--- a/solution.py
+++ b/solution.py
@@ -18,10 +18,8 @@
 SUB = 2
 
 
-def transform_kernel(pitch, begin, gv_ref, go_ref, b_ref, *refs):
-    part, at_sub = pl.program_id(0) + begin, pl.program_id(1)
-    halves = b_ref.shape[2] // LANES
-    out_ref, scratch = refs[-1 - halves], refs[-halves:]
+def transform_kernel(pitch, gv_ref, go_ref, b_ref, out_ref, *scratch):
+    part, at_sub = pl.program_id(0), pl.program_id(1)
     rows = gv_ref.shape[1]
     lam = b_ref.shape[0]
 
@@ -58,50 +56,51 @@
                     out_ref[nb, BAND - 1 - j, to : to + BS, :] = r[row : row + BS]
 
 
-def transform(b, gv, go, cols, which, begin, end, into=None):
+def transform(b, gv, go, cols, which):
     lam, band, _ = b.shape
     nb_total = gv.shape[1] // BS
     rows = NU_PART * BS
     pitch = lam + 2
     subs = NU_PART // SUB
-    held = [] if into is None else [into]
+    parts = nb_total // NU_PART
     return pl.pallas_call(
-        functools.partial(transform_kernel, pitch, begin),
-        grid=(end - begin, subs),
+        functools.partial(transform_kernel, pitch),
+        grid=(parts, subs),
         in_specs=[
-            pl.BlockSpec((lam // BS, rows, band), lambda j, i: (0, j + begin, 0)),
+            pl.BlockSpec((lam // BS, rows, band), lambda j, i: (0, j, 0)),
             pl.BlockSpec(go.shape, lambda j, i: (0, 0)),
             pl.BlockSpec((lam, band, cols), lambda j, i: (0, 0, which)),
-        ]
-        + [pl.BlockSpec(memory_space=pl.ANY)] * len(held),
+        ],
         out_specs=pl.BlockSpec(
-            (SUB, BAND, BS * BS, cols), lambda j, i: ((j + begin) * subs + i, 0, 0, 0)
+            (SUB, BAND, BS * BS, cols), lambda j, i: (j * subs + i, 0, 0, 0)
         ),
         out_shape=jax.ShapeDtypeStruct((nb_total, BAND, BS * BS, cols), jnp.bfloat16),
         scratch_shapes=[pltpu.VMEM((rows * pitch, LANES), jnp.float32)] * (cols // LANES),
-        input_output_aliases={3: 0} if held else {},
         compiler_params=pltpu.CompilerParams(vmem_limit_bytes=62 * 2**20),
         cost_estimate=pl.CostEstimate(
-            flops=75 * 10**8 * (end - begin), bytes_accessed=12 * 2**20, transcendentals=0
+            flops=75 * 10**8 * parts, bytes_accessed=12 * 2**20, transcendentals=0
         ),
         name="transform",
-    )(gv, go, b, *held)
-
-
-def tiles_kernel(masks, halves, nu_ref, code_ref, *refs):
+    )(gv, go, b)
+
+
+def tiles_kernel(masks, halves, code_ref, *refs):
     groups, pairs = len(masks), KB * BAND
     sources, paired = refs[: 2 * groups], refs[2 * groups : 2 * groups + halves]
-    out_ref, tiles, rhs, table, count, tile_sem, pair_sem = refs[-7:]
+    out_ref, tiles, rhs, table, count, jobs, tile_sem, pair_sem = refs[-8:]
     aux = out_ref.shape[0] - 1
     slots = tiles.shape[2]
     cols = rhs.shape[3]
+    group = lax.axis_index("blk")
+    blocks = paired[0].shape[0]
 
     def tile_copy(g, side):
         return pltpu.make_async_copy(sources[2 * g + side], tiles.at[g, side], tile_sem.at[g, side])
 
     def pair_copy(mask, at, p, h):
+        nu = lax.rem((group ^ mask) * KB + p // BAND + p % BAND, blocks)
         return pltpu.make_async_copy(
-            paired[h].at[nu_ref[mask * pairs + p], p % BAND], rhs.at[at, h], pair_sem.at[at, h]
+            paired[h].at[nu, p % BAND], rhs.at[at, h], pair_sem.at[at, h]
         )
 
     for g, mask in enumerate(masks):
@@ -113,6 +112,7 @@
     out_ref[...] = jnp.zeros_like(out_ref)
     for at in range(groups * pairs * 2):
         count[at] = 0
+    jobs[0] = 0
     for g, mask in enumerate(masks):
         for side in range(2):
 
@@ -125,6 +125,11 @@
                     n = count[at]
                     table[at * slots + n] = lax.div(code, pairs) * 256 + s
                     count[at] = n + 1
+
+                    @pl.when((n > 1) & (n % 2 == 0) & ((side == 0) | (count[at - side] <= n)))
+                    def _():
+                        jobs[0] = jobs[0] + 1
+                        jobs[jobs[0]] = at // 2 * 256 + n // 2
 
                 return carry
 
@@ -153,19 +158,15 @@
         for p in range(pairs):
             item(g, g * pairs + p, 0)
 
-    def rest(pair, carry):
-        more = (jnp.maximum(count[2 * pair], count[2 * pair + 1]) + 1) // 2
-
-        def again(i, carry):
-            item(pair // pairs, pair, i)
-            return carry
-
-        return lax.fori_loop(1, more, again, carry)
-
-    lax.fori_loop(0, groups * pairs, rest, 0)
-
-
-def contract(near, far, paired, nu, codes, aux, masks):
+    def again(job, carry):
+        pair = jobs[job] >> 8
+        item(lax.div(pair, pairs), pair, jobs[job] & 255)
+        return carry
+
+    lax.fori_loop(1, jobs[0] + 1, again, 0)
+
+
+def contract(near, far, paired, codes, aux, masks):
     halves = len(paired)
     cols = paired[0].shape[3]
     q = halves * cols
@@ -176,7 +177,7 @@
     return pl.pallas_call(
         functools.partial(tiles_kernel, masks, halves),
         grid_spec=pltpu.PrefetchScalarGridSpec(
-            num_scalar_prefetch=2,
+            num_scalar_prefetch=1,
             grid=(1,),
             in_specs=[far_memory] * (2 * groups + halves),
             out_specs=acc,
@@ -185,6 +186,7 @@
                 pltpu.VMEM((groups * pairs, halves, BS * BS, cols), jnp.bfloat16),
                 pltpu.SMEM((groups * pairs * 2 * slots,), jnp.int32),
                 pltpu.SMEM((groups * pairs * 2,), jnp.int32),
+                pltpu.SMEM((groups * slots + 1,), jnp.int32),
                 pltpu.SemaphoreType.DMA((groups, 2)),
                 pltpu.SemaphoreType.DMA((groups * pairs, halves)),
             ],
@@ -196,7 +198,6 @@
         ),
         name="contract",
     )(
-        nu,
         codes,
         *[side for pair in zip(near, far) for side in pair],
         *paired,
@@ -208,7 +209,6 @@
     group, member = lax.axis_index("blk"), lax.axis_index("grp")
     lam, _, _, q = b3c.shape
     basis, wide = green_virt.shape
-    blocks = basis // BS
     aux = n_blk * PBD
     slots_here = a_tiles.shape[0]
     spread = n_grp // 2
@@ -221,10 +221,19 @@
 
     turned = a_tiles.reshape(slots_here, PB, BS, BS).swapaxes(2, 3).reshape(a_tiles.shape)
 
-    coded = jnp.stack([tile_codes // (KB * BAND), tile_codes % (KB * BAND)])
-    coded = jnp.where(tile_codes >= 0, coded, -1).astype(jnp.bfloat16)
+    per = n_grp // n_blk
+    turn = [
+        (k * n_grp + j, j // per * n_grp + k * per + j % per)
+        for k in range(n_blk)
+        for j in range(n_grp)
+    ]
+    occ_here = lax.ppermute(green_occ, ("blk", "grp"), turn)
+    coded = jnp.stack([tile_codes >> 4, tile_codes & 15]).astype(jnp.bfloat16)
     coded = jnp.pad(coded, ((0, 14), (0, wide - slots_here)))
-    small = jnp.concatenate([green_virt, green_occ, coded], axis=0)[None]
+    coded = [coded if mask == 0 else blk_swap(coded, mask) for mask in range(n_blk)]
+    coded = jnp.concatenate([c[:2] for c in coded], axis=0)
+    coded = jnp.pad(coded, ((0, -coded.shape[0] % 16), (0, 0)))
+    small = jnp.concatenate([green_virt, occ_here, coded], axis=0)[None]
     bit = 2
     while bit < n_grp:
         moved = grp_swap(small, bit)
@@ -235,22 +244,10 @@
     order = relative % 2 * spread + relative // 2
     ordered = jnp.take(small[:, : basis + lam], order, axis=0)
     virt_all = ordered[:, :basis].swapaxes(0, 1).reshape(basis, basis)
-    occ_rows = ordered[:, basis:].swapaxes(0, 1).reshape(lam, basis)
-    code_rows = -(-2 * n_grp * slots_here // (16 * lam)) * 16
-    part = small[:, basis + lam : basis + lam + 2, :slots_here].swapaxes(0, 1).reshape(2, -1)
-    part = jnp.pad(part, ((0, 0), (0, code_rows // 2 * lam - part.shape[1])))
-    part = part.reshape(code_rows, lam)
-    received = []
-    for mask in range(n_blk):
-        mine = lax.dynamic_slice_in_dim(occ_rows, (group ^ mask) * lam, lam, 1)
-        packet = jnp.concatenate([mine, part], axis=0)
-        received.append(blk_swap(packet, mask) if mask else packet)
-    received = jnp.stack(received)
-    occ = jnp.take(received[:, :lam], jnp.arange(n_blk, dtype=jnp.int32) ^ group, axis=0)
-    occ = occ.reshape(basis, lam)
-    part = received[:, lam:].reshape(n_blk, 2, -1)[:, :, : n_grp * slots_here].astype(jnp.int32)
-    codes = jnp.where(part[:, 0] >= 0, part[:, 0] * (KB * BAND) + part[:, 1], -1)
-    codes = codes.reshape(-1)
+    occ = ordered[:, basis:].reshape(n_blk, per, lam, wide).swapaxes(1, 2).reshape(basis, lam)
+    part = small[:, basis + lam : basis + lam + 2 * n_blk, :slots_here].astype(jnp.int32)
+    part = part.reshape(n_grp, n_blk, 2, slots_here)
+    codes = (part[:, :, 0] * 16 + part[:, :, 1]).swapaxes(0, 1).reshape(-1)
 
     mask = lax.dynamic_slice_in_dim(occ_mask, group * KB, KB, 1)
     mask = jnp.repeat(jnp.repeat(mask, BS, axis=0), BS, axis=1).astype(jnp.bfloat16)
@@ -260,29 +257,24 @@
     virt = lax.dynamic_slice_in_dim(virt, group * lam, lam + (BAND - 1) * BS, 1)
     virt = jnp.stack([virt[:, l * BS : (l + BAND) * BS] for l in range(KB)])
 
-    owners = jnp.arange(n_blk, dtype=jnp.int32) ^ group
-    pair = jnp.arange(KB * BAND, dtype=jnp.int32)
-    nu = ((owners[:, None] * KB + (pair // BAND + pair % BAND)[None, :]) % blocks).reshape(-1)
-
     b = b3c.reshape(lam, BAND * BS, q)
     cols = min(2 * LANES, q)
-    parts = blocks // NU_PART
     hops = []
     for d in range(1, spread):
         hops.append(grp_swap(turned, 2 * d))
-    paired = transform(b, virt, occ, cols, 0, 0, 1)
+    paired = [transform(b, virt, occ, cols, 0)]
     hops, paired = lax.optimization_barrier((hops, paired))
     near = {0: jnp.concatenate([turned] + hops)}
     bits = [1 << i for i in range((n_blk - 1).bit_length())]
     for to in bits:
         near[to] = blk_swap(near[0], to)
     far = {0: grp_swap(near[0], 1)}
-    paired = [transform(b, virt, occ, cols, 0, 1, parts, paired)]
-    paired += [transform(b, virt, occ, cols, h, 0, parts) for h in range(1, q // cols)]
-    arriving, paired = lax.optimization_barrier(([[near[to]] for to in bits], paired))
+    paired += [transform(b, virt, occ, cols, h) for h in range(1, q // cols)]
+    chi = contract([near[0]], [far[0]], paired, codes, aux, (0,))
+    arriving, chi = lax.optimization_barrier(([[near[to]] for to in bits], chi))
+    sums = [chi]
     levels = [[m for m in range(n_blk) if m.bit_count() == n] for n in range(1, len(bits) + 1)]
     half = near[0].shape[0] // 2
-    sums, first = [], [0]
     for masks, after in zip(levels, levels[1:] + [[]]):
         for to, pieces in zip(masks, arriving):
             near[to] = pieces[0] if len(pieces) == 1 else jnp.concatenate(pieces)
@@ -294,14 +286,13 @@
             )
         for to in masks:
             far[to] = grp_swap(near[to], 1)
-        now = tuple(first + masks)
-        first = []
-        chi = contract([near[m] for m in now], [far[m] for m in now], paired, nu, codes, aux, now)
+        chi = contract([near[m] for m in masks], [far[m] for m in masks], paired, codes, aux, masks)
         arriving, chi = lax.optimization_barrier((arriving, chi))
-        sums.append(chi[:aux].reshape(n_blk, PBD * PB, q))
+        sums.append(chi)
 
     def piece(d):
-        return sum(lax.dynamic_index_in_dim(chi, group ^ d, 0, False) for chi in sums)
+        rows = [lax.dynamic_slice_in_dim(chi, (group ^ d) * PBD, PBD, 0) for chi in sums]
+        return sum(rows).reshape(PBD * PB, q)
 
     total = piece(0)
     for d in range(1, n_blk):

time: 131 us -> 146 us (1.11)
  starting transfers between devices: 23.7 us -> 46.4 us
  waiting for transfers between devices: 18.4 us -> 13.3 us
  local copies, waits for them, and re-layouts: 17.6 us -> 15.9 us
  Pallas kernels: 64.7 us -> 63.1 us
    ppermute x10, starting transfers between devices: 12.6 us -> 28.9 us  [grp_swap(): return lax.ppermute(a, 'grp', [(i, i ^ bits) for i in range(n_grp)])]
    ppermute x10, starting transfers between devices: 11.2 us -> 16.6 us  [blk_swap(): return lax.ppermute(a, 'blk', [(i, i ^ bits) for i in range(n_blk)])]
    ppermute x10, waiting for transfers between devices: 12.1 us -> 7.77 us  [grp_swap(): return lax.ppermute(a, 'grp', [(i, i ^ bits) for i in range(n_grp)])]
    pallas_call x3 -> x2, Pallas kernels: 37.8 us -> 33.5 us  [transform(): pl.pallas_call(functools.partial(transform_kernel, pitch), grid=(parts, s...]
    pallas_call x2 -> x3, Pallas kernels: 26.9 us -> 29.6 us  [contract(): pl.pallas_call(functools.partial(tiles_kernel, masks, halves), grid_spec=...]
    slice x4 -> x7, local copies, waits for them, and re-layouts: 2.67 us -> 0.17 us  [the longest x1 0.12 us: local(): ordered = jnp.take(small[:, :basis + lam], order, axis=0)]
    convert_element_type x1, other arithmetic: 0.12 us -> 1.81 us  [local(): piece(d).astype(jnp.bfloat16)]
    unnamed x18 -> x22, local copies, waits for them, and re-layouts: 3.72 us -> 4.34 us
  transfers between devices with their start and end apart: 20 -> 21, of which waited for: 7 -> 6; matrix products, arithmetic and copies ran while one was open for 10% -> 9% of each run, Pallas kernels for 43% -> 37%
where the time goes in v1:
time: 146 us
  Pallas kernels  63.1 us (43%)
  starting transfers between devices  46.4 us (32%)
  local copies, waits for them, and re-layouts  15.9 us (11%)
  waiting for transfers between devices  13.3 us (9%)
  other arithmetic  6.36 us (4%)
    pallas_call x2, Pallas kernels, transform(): pl.pallas_call(functools.partial(transform_kernel, pitch), grid=(parts, s...  33.5 us
    pallas_call x3, Pallas kernels, contract(): pl.pallas_call(functools.partial(tiles_kernel, masks, halves), grid_spec=...  29.6 us
    ppermute x10, starting transfers between devices, grp_swap(): return lax.ppermute(a, 'grp', [(i, i ^ bits) for i in range(n_grp)])  28.9 us
    ppermute x10, starting transfers between devices, blk_swap(): return lax.ppermute(a, 'blk', [(i, i ^ bits) for i in range(n_blk)])  16.6 us
    ppermute x10, waiting for transfers between devices, grp_swap(): return lax.ppermute(a, 'grp', [(i, i ^ bits) for i in range(n_grp)])  7.77 us
    ppermute x10, waiting for transfers between devices, blk_swap(): return lax.ppermute(a, 'blk', [(i, i ^ bits) for i in range(n_blk)])  5.52 us
    unnamed x22, local copies, waits for them, and re-layouts  4.34 us
    reshape x3, local copies, waits for them, and re-layouts, local(): a_tiles.reshape(slots_here, PB, BS, BS).swapaxes(2, 3)  3.61 us
  transfers between devices with their start and end apart: 21, of which 6 were waited for; matrix products, arithmetic and copies ran while one was open for 9% of the time, Pallas kernels for 37%

profile of v1, /device:TPU:0, one launch (start us, length us, event | category | flops | bytes accessed | tf_op | source)
XLA Modules:
  0.0 145.5 jit_solution(894059228997640737)
XLA Ops:
  0.7 3.0 %collective-permute-start.4 = (bf16[16,48]{1,0:T(8,128)(2,1)S(1)}, bf16[16,48]{1,0:T(8,128)(2,1)S(1)}, u32[]{:S(2)}, u32[]{:S(2)}) collective-permute-start(bf16[16,48]{1,0:T(8,128)(2,1)S(1)} %fusion.12), channel_id=1, source_target_pairs={{0,8},{8,0},{16,24},{24,16},{1,9},{9,1},{17,25},{25,17},{2,10},{10... | collective-permute-start | bytes 4616 | tf_op jit(solution)/shard_map/ppermute | solution.py:220
  3.7 1.5 %collective-permute-start.5 = (bf16[16,48]{1,0:T(8,128)(2,1)S(1)}, bf16[16,48]{1,0:T(8,128)(2,1)S(1)}, u32[]{:S(2)}, u32[]{:S(2)}) collective-permute-start(bf16[16,48]{1,0:T(8,128)(2,1)S(1)} %fusion.12), channel_id=1, source_target_pairs={{0,16},{8,24},{16,0},{24,8},{1,17},{9,25},{17,1},{25,9},{2,18},{10... | collective-permute-start | bytes 4616 | tf_op jit(solution)/shard_map/ppermute | solution.py:220
  5.3 1.8 %reshape.134 = bf16[4,32,32,32]{3,2,1,0:T(8,128)(2,1)S(1)} reshape(bf16[4,32,1024]{2,1,0:T(8,128)(2,1)} %param.10) | data formatting | bytes 524288 | tf_op jit(solution)/shard_map/reshape | solution.py:222
  7.8 1.1 reshape.135
  8.9 2.1 %collective-permute-start = (bf16[4,32,1024]{2,1,0:T(8,128)(2,1)S(1)}, bf16[4,32,1024]{2,1,0:T(8,128)(2,1)S(1)}, u32[]{:S(2)}, u32[]{:S(2)}) collective-permute-start(bf16[4,32,1024]{2,1,0:T(8,128)(2,1)S(1)} %reshape.135), channel_id=1, source_target_pairs={{0,2},{1,3},{2,0},{3,1},{4,6},{5,7},{6,4},{7,5},{8,10},{9,11},{10,... | collective-permute-start | bytes 786440 | tf_op jit(solution)/shard_map/ppermute | solution.py:217
  11.0 2.6 %collective-permute-start.1 = (bf16[4,32,1024]{2,1,0:T(8,128)(2,1)S(1)}, bf16[4,32,1024]{2,1,0:T(8,128)(2,1)S(1)}, u32[]{:S(2)}, u32[]{:S(2)}) collective-permute-start(bf16[4,32,1024]{2,1,0:T(8,128)(2,1)S(1)} %reshape.135), channel_id=1, source_target_pairs={{0,4},{1,5},{2,6},{3,7},{4,0},{5,1},{6,2},{7,3},{8,12},{9,13},{10,... | collective-permute-start | bytes 786440 | tf_op jit(solution)/shard_map/ppermute | solution.py:217
  13.8 0.8 collective-permute-start.3
  14.9 17.1 %collective-permute-start.7 = (bf16[1,496,48]{1,0,2:T(2,128)(2,1)S(1)}, bf16[1,496,48]{1,0,2:T(2,128)(2,1)S(1)}, u32[]{:S(2)}, u32[]{:S(2)}) collective-permute-start(bf16[1,496,48]{1,0,2:T(2,128)(2,1)S(1)} %copy.40), channel_id=1, source_target_pairs={{0,2},{1,3},{2,0},{3,1},{4,6},{5,7},{6,4},{7,5},{8,10},{9,11},{10,... | collective-permute-start | bytes 142856 | tf_op jit(solution)/shard_map/ppermute | solution.py:217
  32.3 2.4 %collective-permute-done.7 = bf16[1,496,48]{1,0,2:T(2,128)(2,1)S(1)} collective-permute-done((bf16[1,496,48]{1,0,2:T(2,128)(2,1)S(1)}, bf16[1,496,48]{1,0,2:T(2,128)(2,1)S(1)}, u32[]{:S(2)}, u32[]{:S(2)}) %collective-permute-start.7) | collective-permute-done | bytes 47648 | tf_op jit(solution)/shard_map/ppermute | solution.py:217
  34.9 6.3 %collective-permute-start.8 = (bf16[2,496,48]{1,0,2:T(2,128)(2,1)S(1)}, bf16[2,496,48]{1,0,2:T(2,128)(2,1)S(1)}, u32[]{:S(2)}, u32[]{:S(2)}) collective-permute-start(bf16[2,496,48]{1,0,2:T(2,128)(2,1)S(1)} %pad_maximum_fusion.4), channel_id=1, source_target_pairs={{0,4},{1,5},{2,6},{3,7},{4,0},{5,1},{6,2},{7,3},{8,12},{9,13},{10,... | collective-permute-start | bytes 285704 | tf_op jit(solution)/shard_map/ppermute | solution.py:217
  41.3 2.8 %collective-permute-done.8 = bf16[2,496,48]{1,0,2:T(2,128)(2,1)S(1)} collective-permute-done((bf16[2,496,48]{1,0,2:T(2,128)(2,1)S(1)}, bf16[2,496,48]{1,0,2:T(2,128)(2,1)S(1)}, u32[]{:S(2)}, u32[]{:S(2)}) %collective-permute-start.8) | collective-permute-done | bytes 95264 | tf_op jit(solution)/shard_map/ppermute | solution.py:217
  48.9 0.8 pad_maximum_fusion.1.gv_ref
  49.7 16.7 %transform.2.refs_2_.refs_4_ = bf16[12,3,1024,256]{3,2,1,0:T(8,128)(2,1)} custom-call(bf16[3,384,96]{2,1,0:T(8,128)(2,1)} %pad_maximum_fusion.1.gv_ref, bf16[448,96]{1,0:T(8,128)(2,1)} %pad_maximum_fusion.3.go_ref, bf16[96,96,512]{2,1,0:T(8,128)(2,1)} %bitcast.55), custom_call_target="tpu_custom_call" | custom-call | flops 15000000512 | bytes 12582912 | tf_op jit(solution)/shard_map/transform/pallas_call | solution.py:66
  67.8 1.7 %constant_dynamic-update-slice_fusion.refs_0_ = bf16[16,32,1024]{2,1,0:T(8,128)(2,1)} fusion(bf16[16,32,1024]{2,1,0:T(8,128)(2,1)} %constant_dynamic-update-slice_fusion.1, bf16[4,32,1024]{2,1,0:T(8,128)(2,1)} %collective-permute-done.2), kind=kLoop, calls=%fused_computation.26 | loop fusion | bytes 524288 | tf_op jit(solution)/shard_map/concatenate | solution.py:267
  69.7 5.9 %collective-permute-start.10 = (bf16[16,32,1024]{2,1,0:T(8,128)(2,1)}, bf16[16,32,1024]{2,1,0:T(8,128)(2,1)S(1)}, u32[]{:S(2)}, u32[]{:S(2)}) collective-permute-start(bf16[16,32,1024]{2,1,0:T(8,128)(2,1)} %constant_dynamic-update-slice_fusion.refs_0_), channel_id=1, source_target_pairs={{0,8},{8,0},{16,24},{24,16},{1,9},{9,1},{17,25},{25,17},{2,10},{10... | collective-permute-start | bytes 3145736 | tf_op jit(solution)/shard_map/ppermute | solution.py:220
  75.6 16.8 %transform.3.refs_3_.refs_5_ = bf16[12,3,1024,256]{3,2,1,0:T(8,128)(2,1)} custom-call(bf16[3,384,96]{2,1,0:T(8,128)(2,1)} %pad_maximum_fusion.1.gv_ref, bf16[448,96]{1,0:T(8,128)(2,1)} %pad_maximum_fusion.3.go_ref, bf16[96,96,512]{2,1,0:T(8,128)(2,1)} %bitcast.56), custom_call_target="tpu_custom_call" | custom-call | flops 15000000512 | bytes 12582912 | tf_op jit(solution)/shard_map/transform/pallas_call | solution.py:66
  93.3 8.4 %contract.3 = f32[17,32,512]{2,1,0:T(8,128)} custom-call(s32[128]{0:T(128)} %reshape.142.code_ref, bf16[16,32,1024]{2,1,0:T(8,128)(2,1)} %constant_dynamic-update-slice_fusion.refs_0_, bf16[16,32,1024]{2,1,0:T(8,128)(2,1)} %collective-permute-done.12.refs_1_, bf16[12,3,1024,256]{3,2,1,0:T(8,128)(2,1)} %transform.2.refs_2_.refs_4_, ...), custom_call_target="tpu_custom_call" | custom-call | flops 4000000000 | bytes 12582912 | tf_op jit(solution)/shard_map/contract/pallas_call | solution.py:177
  102.3 1.9 %slice.66 = bf16[8,32,1024]{2,1,0:T(8,128)(2,1)} slice(bf16[16,32,1024]{2,1,0:T(8,128)(2,1)} %collective-permute-done.11.refs_2_), slice={[0:8], [0:32], [0:1024]} | slice | bytes 1048576 | tf_op jit(solution)/shard_map/slice | solution.py:285
  104.2 0.8 slice.67
  105.0 1.0 collective-permute-start.13
  106.0 1.6 %collective-permute-start.14 = (bf16[8,32,1024]{2,1,0:T(8,128)(2,1)}, bf16[8,32,1024]{2,1,0:T(8,128)(2,1)}, u32[]{:S(2)}, u32[]{:S(2)}) collective-permute-start(bf16[8,32,1024]{2,1,0:T(8,128)(2,1)} %slice.67), channel_id=1, source_target_pairs={{0,16},{8,24},{16,0},{24,8},{1,17},{9,25},{17,1},{25,9},{2,18},{10... | collective-permute-start | bytes 1572872 | tf_op jit(solution)/shard_map/ppermute | solution.py:220
  107.6 1.0 copy-done.5
  108.6 12.5 %contract.4 = f32[17,32,512]{2,1,0:T(8,128)} custom-call(s32[128]{0:T(128)} %reshape.142.code_ref, bf16[16,32,1024]{2,1,0:T(8,128)(2,1)} %copy-done.3, bf16[16,32,1024]{2,1,0:T(8,128)(2,1)} %copy-done.5, bf16[16,32,1024]{2,1,0:T(8,128)(2,1)} %collective-permute-done.11.refs_2_, bf16[16,32,1024]{2,1,0:T(8,128)(2,1)} %collective-permute-done.16.refs_3_, ...), custom_call_target="tpu_custom_call" | custom-call | flops 8000000000 | bytes 25165824 | tf_op jit(solution)/shard_map/contract/pallas_call | solution.py:177
  121.2 1.1 constant_dynamic-update-slice_fusion.4.refs_0_
  122.4 0.9 copy-done.4
  123.3 1.9 %collective-permute-done.17.refs_1_ = bf16[16,32,1024]{2,1,0:T(8,128)(2,1)} collective-permute-done((bf16[16,32,1024]{2,1,0:T(8,128)(2,1)S(1)}, bf16[16,32,1024]{2,1,0:T(8,128)(2,1)}, u32[]{:S(2)}, u32[]{:S(2)}) %collective-permute-start.17) | collective-permute-done | bytes 1048608 | tf_op jit(solution)/shard_map/ppermute | solution.py:217
  125.1 8.7 %contract.5 = f32[17,32,512]{2,1,0:T(8,128)} custom-call(s32[128]{0:T(128)} %reshape.142.code_ref, bf16[16,32,1024]{2,1,0:T(8,128)(2,1)} %copy-done.4, bf16[16,32,1024]{2,1,0:T(8,128)(2,1)} %collective-permute-done.17.refs_1_, bf16[12,3,1024,256]{3,2,1,0:T(8,128)(2,1)} %transform.2.refs_2_.refs_4_, bf16[12,3,1024,256]{3,2,1,0:T(8,128)(2,1)} %transform.3.refs_3_.refs_5_), custom_call_target="tpu_custom_call" | custom-call | flops 4000000000 | bytes 12582912 | tf_op jit(solution)/shard_map/contract/pallas_call | solution.py:177
  133.9 1.8 %add_convert_fusion.2 = (bf16[4,32,512]{2,1,0:T(8,128)(2,1)S(1)}, bf16[4,32,512]{2,1,0:T(8,128)(2,1)S(1)}, bf16[4,32,512]{2,1,0:T(8,128)(2,1)S(1)}, f32[4,32,512]{2,1,0:T(8,128)S(1)}) fusion(f32[17,32,512]{2,1,0:T(8,128)} %contract.5, s32[]{:T(128)S(6)} %select_n.89, f32[17,32,512]{2,1,0:T(8,128)} %contract.4, f32[17,32,512]{2,1,0:T(8,128)S(1)} %copy-done.2, ...), kind=kLoop, calls=%fused_computation.11 | loop fusion | flops 720896 | bytes 3801104 | tf_op jit(solution)/shard_map/convert_element_type | solution.py:299
  135.7 1.0 collective-permute-start.18
  137.0 2.2 %collective-permute-start.20 = (bf16[128,512]{1,0:T(8,128)(2,1)S(1)}, bf16[128,512]{1,0:T(8,128)(2,1)S(1)}, u32[]{:S(2)}, u32[]{:S(2)}) collective-permute-start(bf16[128,512]{1,0:T(8,128)(2,1)S(1)} %bitcast.51), channel_id=1, source_target_pairs={{0,24},{8,16},{16,8},{24,0},{1,25},{9,17},{17,9},{25,1},{2,26},{10... | collective-permute-start | bytes 393224 | tf_op jit(solution)/shard_map/ppermute | solution.py:220
  139.3 2.9 %collective-permute-done.18 = bf16[128,512]{1,0:T(8,128)(2,1)S(1)} collective-permute-done((bf16[128,512]{1,0:T(8,128)(2,1)S(1)}, bf16[128,512]{1,0:T(8,128)(2,1)S(1)}, u32[]{:S(2)}, u32[]{:S(2)}) %collective-permute-start.18) | collective-permute-done | bytes 131104 | tf_op jit(solution)/shard_map/ppermute | solution.py:220
  142.1 2.6 %collective-permute-done.19 = bf16[128,512]{1,0:T(8,128)(2,1)S(1)} collective-permute-done((bf16[128,512]{1,0:T(8,128)(2,1)S(1)}, bf16[128,512]{1,0:T(8,128)(2,1)S(1)}, u32[]{:S(2)}, u32[]{:S(2)}) %collective-permute-start.19) | collective-permute-done | bytes 131104 | tf_op jit(solution)/shard_map/ppermute | solution.py:220
  (87 shorter events, 11.3 us)
Async XLA Ops:
  0.0 13.6 %copy-start = (s32[12,12]{1,0:T(8,128)S(1)}, s32[12,12]{1,0:T(8,128)}, u32[]{:S(2)}) copy-start(s32[12,12]{1,0:T(8,128)} %param.9) | copy-start | bytes 1732
  0.7 13.0 %collective-permute-start.4 = (bf16[16,48]{1,0:T(8,128)(2,1)S(1)}, bf16[16,48]{1,0:T(8,128)(2,1)S(1)}, u32[]{:S(2)}, u32[]{:S(2)}) collective-permute-start(bf16[16,48]{1,0:T(8,128)(2,1)S(1)} %fusion.12), channel_id=1, source_target_pairs={{0,8},{8,0},{16,24},{24,16},{1,9},{9,1},{17,25},{25,17},{2,10},{10... | collective-permute-start | bytes 4616 | tf_op jit(solution)/shard_map/ppermute | solution.py:220
  3.7 10.0 %collective-permute-start.5 = (bf16[16,48]{1,0:T(8,128)(2,1)S(1)}, bf16[16,48]{1,0:T(8,128)(2,1)S(1)}, u32[]{:S(2)}, u32[]{:S(2)}) collective-permute-start(bf16[16,48]{1,0:T(8,128)(2,1)S(1)} %fusion.12), channel_id=1, source_target_pairs={{0,16},{8,24},{16,0},{24,8},{1,17},{9,25},{17,1},{25,9},{2,18},{10... | collective-permute-start | bytes 4616 | tf_op jit(solution)/shard_map/ppermute | solution.py:220
  5.2 9.4 %collective-permute-start.6 = (bf16[16,48]{1,0:T(8,128)(2,1)S(1)}, bf16[16,48]{1,0:T(8,128)(2,1)S(1)}, u32[]{:S(2)}, u32[]{:S(2)}) collective-permute-start(bf16[16,48]{1,0:T(8,128)(2,1)S(1)} %fusion.12), channel_id=1, source_target_pairs={{0,24},{8,16},{16,8},{24,0},{1,25},{9,17},{17,9},{25,1},{2,26},{10... | collective-permute-start | bytes 4616 | tf_op jit(solution)/shard_map/ppermute | solution.py:220
  7.7 6.0 %copy-start.7 = (bf16[96,48]{0,1:T(8,128)(2,1)S(1)}, bf16[96,48]{0,1:T(8,128)(2,1)}, u32[]{:S(2)}) copy-start(bf16[96,48]{0,1:T(8,128)(2,1)} %param.7) | copy-start | bytes 27652
  7.8 7.0 %copy-start.6 = (bf16[384,48]{0,1:T(8,128)(2,1)S(1)}, bf16[384,48]{0,1:T(8,128)(2,1)}, u32[]{:S(2)}) copy-start(bf16[384,48]{0,1:T(8,128)(2,1)} %param.8) | copy-start | bytes 110596
  8.9 57.5 %collective-permute-start = (bf16[4,32,1024]{2,1,0:T(8,128)(2,1)S(1)}, bf16[4,32,1024]{2,1,0:T(8,128)(2,1)S(1)}, u32[]{:S(2)}, u32[]{:S(2)}) collective-permute-start(bf16[4,32,1024]{2,1,0:T(8,128)(2,1)S(1)} %reshape.135), channel_id=1, source_target_pairs={{0,2},{1,3},{2,0},{3,1},{4,6},{5,7},{6,4},{7,5},{8,10},{9,11},{10,... | collective-permute-start | bytes 786440 | tf_op jit(solution)/shard_map/ppermute | solution.py:217
  11.0 55.4 %collective-permute-start.1 = (bf16[4,32,1024]{2,1,0:T(8,128)(2,1)S(1)}, bf16[4,32,1024]{2,1,0:T(8,128)(2,1)S(1)}, u32[]{:S(2)}, u32[]{:S(2)}) collective-permute-start(bf16[4,32,1024]{2,1,0:T(8,128)(2,1)S(1)} %reshape.135), channel_id=1, source_target_pairs={{0,4},{1,5},{2,6},{3,7},{4,0},{5,1},{6,2},{7,3},{8,12},{9,13},{10,... | collective-permute-start | bytes 786440 | tf_op jit(solution)/shard_map/ppermute | solution.py:217
  13.7 52.7 %collective-permute-start.2 = (bf16[4,32,1024]{2,1,0:T(8,128)(2,1)S(1)}, bf16[4,32,1024]{2,1,0:T(8,128)(2,1)}, u32[]{:S(2)}, u32[]{:S(2)}) collective-permute-start(bf16[4,32,1024]{2,1,0:T(8,128)(2,1)S(1)} %reshape.135), channel_id=1, source_target_pairs={{0,6},{1,7},{2,4},{3,5},{4,2},{5,3},{6,0},{7,1},{8,14},{9,15},{10,... | collective-permute-start | bytes 786440 | tf_op jit(solution)/shard_map/ppermute | solution.py:217
  13.8 1.0 collective-permute-start.3
  14.9 19.8 %collective-permute-start.7 = (bf16[1,496,48]{1,0,2:T(2,128)(2,1)S(1)}, bf16[1,496,48]{1,0,2:T(2,128)(2,1)S(1)}, u32[]{:S(2)}, u32[]{:S(2)}) collective-permute-start(bf16[1,496,48]{1,0,2:T(2,128)(2,1)S(1)} %copy.40), channel_id=1, source_target_pairs={{0,2},{1,3},{2,0},{3,1},{4,6},{5,7},{6,4},{7,5},{8,10},{9,11},{10,... | collective-permute-start | bytes 142856 | tf_op jit(solution)/shard_map/ppermute | solution.py:217
  34.9 9.1 %collective-permute-start.8 = (bf16[2,496,48]{1,0,2:T(2,128)(2,1)S(1)}, bf16[2,496,48]{1,0,2:T(2,128)(2,1)S(1)}, u32[]{:S(2)}, u32[]{:S(2)}) collective-permute-start(bf16[2,496,48]{1,0,2:T(2,128)(2,1)S(1)} %pad_maximum_fusion.4), channel_id=1, source_target_pairs={{0,4},{1,5},{2,6},{3,7},{4,0},{5,1},{6,2},{7,3},{8,12},{9,13},{10,... | collective-permute-start | bytes 285704 | tf_op jit(solution)/shard_map/ppermute | solution.py:217
  44.4 1.5 %collective-permute-start.9 = (bf16[4,496,48]{1,0,2:T(4,128)(2,1)S(1)}, bf16[4,496,48]{1,0,2:T(4,128)(2,1)S(1)}, u32[]{:S(2)}, u32[]{:S(2)}) collective-permute-start(bf16[4,496,48]{1,0,2:T(4,128)(2,1)S(1)} %pad_maximum_fusion.2), channel_id=1, source_target_pairs={{0,1},{1,0},{2,3},{3,2},{4,5},{5,4},{6,7},{7,6},{8,9},{9,8},{10,11... | collective-permute-start | bytes 571400 | tf_op jit(solution)/shard_map/ppermute | solution.py:217
  69.5 23.7 %collective-permute-start.12 = (bf16[16,32,1024]{2,1,0:T(8,128)(2,1)}, bf16[16,32,1024]{2,1,0:T(8,128)(2,1)}, u32[]{:S(2)}, u32[]{:S(2)}) collective-permute-start(bf16[16,32,1024]{2,1,0:T(8,128)(2,1)} %constant_dynamic-update-slice_fusion.refs_0_), channel_id=1, source_target_pairs={{0,1},{1,0},{2,3},{3,2},{4,5},{5,4},{6,7},{7,6},{8,9},{9,8},{10,11... | collective-permute-start | bytes 3145736 | tf_op jit(solution)/shard_map/ppermute | solution.py:217
  69.7 32.0 %collective-permute-start.10 = (bf16[16,32,1024]{2,1,0:T(8,128)(2,1)}, bf16[16,32,1024]{2,1,0:T(8,128)(2,1)S(1)}, u32[]{:S(2)}, u32[]{:S(2)}) collective-permute-start(bf16[16,32,1024]{2,1,0:T(8,128)(2,1)} %constant_dynamic-update-slice_fusion.refs_0_), channel_id=1, source_target_pairs={{0,8},{8,0},{16,24},{24,16},{1,9},{9,1},{17,25},{25,17},{2,10},{10... | collective-permute-start | bytes 3145736 | tf_op jit(solution)/shard_map/ppermute | solution.py:220
  75.6 26.2 %collective-permute-start.11 = (bf16[16,32,1024]{2,1,0:T(8,128)(2,1)}, bf16[16,32,1024]{2,1,0:T(8,128)(2,1)}, u32[]{:S(2)}, u32[]{:S(2)}) collective-permute-start(bf16[16,32,1024]{2,1,0:T(8,128)(2,1)} %constant_dynamic-update-slice_fusion.refs_0_), channel_id=1, source_target_pairs={{0,16},{8,24},{16,0},{24,8},{1,17},{9,25},{17,1},{25,9},{2,18},{10... | collective-permute-start | bytes 3145736 | tf_op jit(solution)/shard_map/ppermute | solution.py:220
  101.7 6.9 %copy-start.3 = (bf16[16,32,1024]{2,1,0:T(8,128)(2,1)}, bf16[16,32,1024]{2,1,0:T(8,128)(2,1)S(1)}, u32[]{:S(2)}) copy-start(bf16[16,32,1024]{2,1,0:T(8,128)(2,1)S(1)} %collective-permute-done.10.refs_0_) | copy-start | bytes 3145732
  101.7 5.9 %collective-permute-start.15 = (bf16[16,32,1024]{2,1,0:T(8,128)(2,1)S(1)}, bf16[16,32,1024]{2,1,0:T(8,128)(2,1)S(1)}, u32[]{:S(2)}, u32[]{:S(2)}) collective-permute-start(bf16[16,32,1024]{2,1,0:T(8,128)(2,1)S(1)} %collective-permute-done.10.refs_0_), channel_id=1, source_target_pairs={{0,1},{1,0},{2,3},{3,2},{4,5},{5,4},{6,7},{7,6},{8,9},{9,8},{10,11... | collective-permute-start | bytes 3145736 | tf_op jit(solution)/shard_map/ppermute | solution.py:217
  101.9 6.7 %collective-permute-start.16 = (bf16[16,32,1024]{2,1,0:T(8,128)(2,1)}, bf16[16,32,1024]{2,1,0:T(8,128)(2,1)}, u32[]{:S(2)}, u32[]{:S(2)}) collective-permute-start(bf16[16,32,1024]{2,1,0:T(8,128)(2,1)} %collective-permute-done.11.refs_2_), channel_id=1, source_target_pairs={{0,1},{1,0},{2,3},{3,2},{4,5},{5,4},{6,7},{7,6},{8,9},{9,8},{10,11... | collective-permute-start | bytes 3145736 | tf_op jit(solution)/shard_map/ppermute | solution.py:217
  105.0 16.1 %collective-permute-start.13 = (bf16[8,32,1024]{2,1,0:T(8,128)(2,1)}, bf16[8,32,1024]{2,1,0:T(8,128)(2,1)S(1)}, u32[]{:S(2)}, u32[]{:S(2)}) collective-permute-start(bf16[8,32,1024]{2,1,0:T(8,128)(2,1)} %slice.66), channel_id=1, source_target_pairs={{0,8},{8,0},{16,24},{24,16},{1,9},{9,1},{17,25},{25,17},{2,10},{10... | collective-permute-start | bytes 1572872 | tf_op jit(solution)/shard_map/ppermute | solution.py:220
  106.0 15.1 %collective-permute-start.14 = (bf16[8,32,1024]{2,1,0:T(8,128)(2,1)}, bf16[8,32,1024]{2,1,0:T(8,128)(2,1)}, u32[]{:S(2)}, u32[]{:S(2)}) collective-permute-start(bf16[8,32,1024]{2,1,0:T(8,128)(2,1)} %slice.67), channel_id=1, source_target_pairs={{0,16},{8,24},{16,0},{24,8},{1,17},{9,25},{17,1},{25,9},{2,18},{10... | collective-permute-start | bytes 1572872 | tf_op jit(solution)/shard_map/ppermute | solution.py:220
  107.6 1.0 copy-start.5
  122.3 1.0 copy-start.4
  122.3 2.9 %collective-permute-start.17 = (bf16[16,32,1024]{2,1,0:T(8,128)(2,1)S(1)}, bf16[16,32,1024]{2,1,0:T(8,128)(2,1)}, u32[]{:S(2)}, u32[]{:S(2)}) collective-permute-start(bf16[16,32,1024]{2,1,0:T(8,128)(2,1)S(1)} %constant_dynamic-update-slice_fusion.4.refs_0_), channel_id=1, source_target_pairs={{0,1},{1,0},{2,3},{3,2},{4,5},{5,4},{6,7},{7,6},{8,9},{9,8},{10,11... | collective-permute-start | bytes 3145736 | tf_op jit(solution)/shard_map/ppermute | solution.py:217
  123.3 10.6 %copy-start.2 = (f32[17,32,512]{2,1,0:T(8,128)S(1)}, f32[17,32,512]{2,1,0:T(8,128)}, u32[]{:S(2)}) copy-start(f32[17,32,512]{2,1,0:T(8,128)} %contract.3) | copy-start | bytes 3342340
  133.9 11.7 %copy-start.1 = (s32[12,12]{1,0:T(8,128)S(1)}, s32[12,12]{1,0:T(8,128)}, u32[]{:S(2)}) copy-start(s32[12,12]{1,0:T(8,128)} %param.9) | copy-start | bytes 1732
  135.7 6.4 %collective-permute-start.18 = (bf16[128,512]{1,0:T(8,128)(2,1)S(1)}, bf16[128,512]{1,0:T(8,128)(2,1)S(1)}, u32[]{:S(2)}, u32[]{:S(2)}) collective-permute-start(bf16[128,512]{1,0:T(8,128)(2,1)S(1)} %bitcast.53), channel_id=1, source_target_pairs={{0,8},{8,0},{16,24},{24,16},{1,9},{9,1},{17,25},{25,17},{2,10},{10... | collective-permute-start | bytes 393224 | tf_op jit(solution)/shard_map/ppermute | solution.py:220
  136.7 8.1 %collective-permute-start.19 = (bf16[128,512]{1,0:T(8,128)(2,1)S(1)}, bf16[128,512]{1,0:T(8,128)(2,1)S(1)}, u32[]{:S(2)}, u32[]{:S(2)}) collective-permute-start(bf16[128,512]{1,0:T(8,128)(2,1)S(1)} %bitcast.52), channel_id=1, source_target_pairs={{0,16},{8,24},{16,0},{24,8},{1,17},{9,25},{17,1},{25,9},{2,18},{10... | collective-permute-start | bytes 393224 | tf_op jit(solution)/shard_map/ppermute | solution.py:220
  137.0 7.7 %collective-permute-start.20 = (bf16[128,512]{1,0:T(8,128)(2,1)S(1)}, bf16[128,512]{1,0:T(8,128)(2,1)S(1)}, u32[]{:S(2)}, u32[]{:S(2)}) collective-permute-start(bf16[128,512]{1,0:T(8,128)(2,1)S(1)} %bitcast.51), channel_id=1, source_target_pairs={{0,24},{8,16},{16,8},{24,0},{1,25},{9,17},{17,9},{25,1},{2,26},{10... | collective-permute-start | bytes 393224 | tf_op jit(solution)/shard_map/ppermute | solution.py:220

commit v2 on v0

--- a/solution.py
+++ b/solution.py
@@ -88,20 +88,23 @@
     )(gv, go, b, *held)
 
 
-def tiles_kernel(masks, halves, nu_ref, code_ref, *refs):
+def tiles_kernel(masks, halves, code_ref, *refs):
     groups, pairs = len(masks), KB * BAND
     sources, paired = refs[: 2 * groups], refs[2 * groups : 2 * groups + halves]
-    out_ref, tiles, rhs, table, count, tile_sem, pair_sem = refs[-7:]
+    out_ref, tiles, rhs, table, count, jobs, tile_sem, pair_sem = refs[-8:]
     aux = out_ref.shape[0] - 1
     slots = tiles.shape[2]
     cols = rhs.shape[3]
+    group = lax.axis_index("blk")
+    blocks = paired[0].shape[0]
 
     def tile_copy(g, side):
         return pltpu.make_async_copy(sources[2 * g + side], tiles.at[g, side], tile_sem.at[g, side])
 
     def pair_copy(mask, at, p, h):
+        nu = lax.rem((group ^ mask) * KB + p // BAND + p % BAND, blocks)
         return pltpu.make_async_copy(
-            paired[h].at[nu_ref[mask * pairs + p], p % BAND], rhs.at[at, h], pair_sem.at[at, h]
+            paired[h].at[nu, p % BAND], rhs.at[at, h], pair_sem.at[at, h]
         )
 
     for g, mask in enumerate(masks):
@@ -113,6 +116,7 @@
     out_ref[...] = jnp.zeros_like(out_ref)
     for at in range(groups * pairs * 2):
         count[at] = 0
+    jobs[0] = 0
     for g, mask in enumerate(masks):
         for side in range(2):
 
@@ -125,6 +129,11 @@
                     n = count[at]
                     table[at * slots + n] = lax.div(code, pairs) * 256 + s
                     count[at] = n + 1
+
+                    @pl.when((n > 1) & (n % 2 == 0) & ((side == 0) | (count[at - side] <= n)))
+                    def _():
+                        jobs[0] = jobs[0] + 1
+                        jobs[jobs[0]] = at // 2 * 256 + n // 2
 
                 return carry
 
@@ -153,19 +162,15 @@
         for p in range(pairs):
             item(g, g * pairs + p, 0)
 
-    def rest(pair, carry):
-        more = (jnp.maximum(count[2 * pair], count[2 * pair + 1]) + 1) // 2
-
-        def again(i, carry):
-            item(pair // pairs, pair, i)
-            return carry
-
-        return lax.fori_loop(1, more, again, carry)
-
-    lax.fori_loop(0, groups * pairs, rest, 0)
-
-
-def contract(near, far, paired, nu, codes, aux, masks):
+    def again(job, carry):
+        pair = jobs[job] >> 8
+        item(lax.div(pair, pairs), pair, jobs[job] & 255)
+        return carry
+
+    lax.fori_loop(1, jobs[0] + 1, again, 0)
+
+
+def contract(near, far, paired, codes, aux, masks):
     halves = len(paired)
     cols = paired[0].shape[3]
     q = halves * cols
@@ -176,7 +181,7 @@
     return pl.pallas_call(
         functools.partial(tiles_kernel, masks, halves),
         grid_spec=pltpu.PrefetchScalarGridSpec(
-            num_scalar_prefetch=2,
+            num_scalar_prefetch=1,
             grid=(1,),
             in_specs=[far_memory] * (2 * groups + halves),
             out_specs=acc,
@@ -185,6 +190,7 @@
                 pltpu.VMEM((groups * pairs, halves, BS * BS, cols), jnp.bfloat16),
                 pltpu.SMEM((groups * pairs * 2 * slots,), jnp.int32),
                 pltpu.SMEM((groups * pairs * 2,), jnp.int32),
+                pltpu.SMEM((groups * slots + 1,), jnp.int32),
                 pltpu.SemaphoreType.DMA((groups, 2)),
                 pltpu.SemaphoreType.DMA((groups * pairs, halves)),
             ],
@@ -196,7 +202,6 @@
         ),
         name="contract",
     )(
-        nu,
         codes,
         *[side for pair in zip(near, far) for side in pair],
         *paired,
@@ -221,8 +226,7 @@
 
     turned = a_tiles.reshape(slots_here, PB, BS, BS).swapaxes(2, 3).reshape(a_tiles.shape)
 
-    coded = jnp.stack([tile_codes // (KB * BAND), tile_codes % (KB * BAND)])
-    coded = jnp.where(tile_codes >= 0, coded, -1).astype(jnp.bfloat16)
+    coded = jnp.stack([tile_codes >> 4, tile_codes & 15]).astype(jnp.bfloat16)
     coded = jnp.pad(coded, ((0, 14), (0, wide - slots_here)))
     small = jnp.concatenate([green_virt, green_occ, coded], axis=0)[None]
     bit = 2
@@ -249,8 +253,7 @@
     occ = jnp.take(received[:, :lam], jnp.arange(n_blk, dtype=jnp.int32) ^ group, axis=0)
     occ = occ.reshape(basis, lam)
     part = received[:, lam:].reshape(n_blk, 2, -1)[:, :, : n_grp * slots_here].astype(jnp.int32)
-    codes = jnp.where(part[:, 0] >= 0, part[:, 0] * (KB * BAND) + part[:, 1], -1)
-    codes = codes.reshape(-1)
+    codes = (part[:, 0] * 16 + part[:, 1]).reshape(-1)
 
     mask = lax.dynamic_slice_in_dim(occ_mask, group * KB, KB, 1)
     mask = jnp.repeat(jnp.repeat(mask, BS, axis=0), BS, axis=1).astype(jnp.bfloat16)
@@ -260,48 +263,35 @@
     virt = lax.dynamic_slice_in_dim(virt, group * lam, lam + (BAND - 1) * BS, 1)
     virt = jnp.stack([virt[:, l * BS : (l + BAND) * BS] for l in range(KB)])
 
-    owners = jnp.arange(n_blk, dtype=jnp.int32) ^ group
-    pair = jnp.arange(KB * BAND, dtype=jnp.int32)
-    nu = ((owners[:, None] * KB + (pair // BAND + pair % BAND)[None, :]) % blocks).reshape(-1)
-
     b = b3c.reshape(lam, BAND * BS, q)
     cols = min(2 * LANES, q)
-    parts = blocks // NU_PART
     hops = []
     for d in range(1, spread):
         hops.append(grp_swap(turned, 2 * d))
     paired = transform(b, virt, occ, cols, 0, 0, 1)
     hops, paired = lax.optimization_barrier((hops, paired))
     near = {0: jnp.concatenate([turned] + hops)}
-    bits = [1 << i for i in range((n_blk - 1).bit_length())]
-    for to in bits:
+    for to in range(1, n_blk):
         near[to] = blk_swap(near[0], to)
-    far = {0: grp_swap(near[0], 1)}
-    paired = [transform(b, virt, occ, cols, 0, 1, parts, paired)]
-    paired += [transform(b, virt, occ, cols, h, 0, parts) for h in range(1, q // cols)]
-    arriving, paired = lax.optimization_barrier(([[near[to]] for to in bits], paired))
-    levels = [[m for m in range(n_blk) if m.bit_count() == n] for n in range(1, len(bits) + 1)]
-    half = near[0].shape[0] // 2
-    sums, first = [], [0]
-    for masks, after in zip(levels, levels[1:] + [[]]):
-        for to, pieces in zip(masks, arriving):
-            near[to] = pieces[0] if len(pieces) == 1 else jnp.concatenate(pieces)
-        arriving = []
-        for to in after:
-            low, high = to & -to, 1 << (to.bit_length() - 1)
-            arriving.append(
-                [blk_swap(near[to ^ low][:half], low), blk_swap(near[to ^ high][half:], high)]
-            )
-        for to in masks:
-            far[to] = grp_swap(near[to], 1)
-        now = tuple(first + masks)
-        first = []
-        chi = contract([near[m] for m in now], [far[m] for m in now], paired, nu, codes, aux, now)
-        arriving, chi = lax.optimization_barrier((arriving, chi))
-        sums.append(chi[:aux].reshape(n_blk, PBD * PB, q))
+    paired = [transform(b, virt, occ, cols, 0, 1, blocks // NU_PART, paired)]
+    for h in range(1, q // cols):
+        paired.append(transform(b, virt, occ, cols, h, 0, blocks // NU_PART))
+    sums = []
+    for at in range(0, n_blk, 3):
+        masks = range(at, min(at + 3, n_blk))
+        mine = [near[m] for m in masks]
+        if sums:
+            mine, sums[-1] = lax.optimization_barrier((mine, sums[-1]))
+            far = []
+        else:
+            far = [grp_swap(mine[0], 1)]
+            mine[1:], paired = lax.optimization_barrier((mine[1:], paired))
+        far += [grp_swap(tiles, 1) for tiles in mine[len(far) :]]
+        sums.append(contract(mine, far, paired, codes, aux, masks))
 
     def piece(d):
-        return sum(lax.dynamic_index_in_dim(chi, group ^ d, 0, False) for chi in sums)
+        rows = [lax.dynamic_slice_in_dim(chi, (group ^ d) * PBD, PBD, 0) for chi in sums]
+        return sum(rows).reshape(PBD * PB, q)
 
     total = piece(0)
     for d in range(1, n_blk):

time: 131 us -> 131 us (level)
  waiting for transfers between devices: 18.4 us -> 28.9 us
  local copies, waits for them, and re-layouts: 17.6 us -> 8.29 us
    ppermute x10, waiting for transfers between devices: 12.1 us -> 18.5 us  [grp_swap(): return lax.ppermute(a, 'grp', [(i, i ^ bits) for i in range(n_grp)])]
    slice x4 -> x0, local copies, waits for them, and re-layouts: 5.32 us -> none  [the longest x2 2.64 us: local(): sums.append(chi[:aux].reshape(n_blk, PBD * PB, q))]
    ppermute x10 -> x9, waiting for transfers between devices: 6.27 us -> 10.5 us  [blk_swap(): return lax.ppermute(a, 'blk', [(i, i ^ bits) for i in range(n_blk)])]
    unnamed x18 -> x25, local copies, waits for them, and re-layouts: 3.72 us -> 1.66 us
    ppermute x10 -> x9, starting transfers between devices: 11.2 us -> 10.6 us  [blk_swap(): return lax.ppermute(a, 'blk', [(i, i ^ bits) for i in range(n_blk)])]
  transfers between devices with their start and end apart: 20 -> 19, of which waited for: 7 -> 10; matrix products, arithmetic and copies ran while one was open for 10% -> 6% of each run, Pallas kernels for 43% -> 42%
where the time goes in v2:
time: 131 us; the launch traced here: 130 us
  Pallas kernels  63.8 us (49%)
  waiting for transfers between devices  28.9 us (22%)
  starting transfers between devices  23 us (18%)
  local copies, waits for them, and re-layouts  8.29 us (6%)
  other arithmetic  5.93 us (5%)
    pallas_call x3, Pallas kernels, transform(): pl.pallas_call(functools.partial(transform_kernel, pitch, begin), grid=(e...  37.8 us
    pallas_call x2, Pallas kernels, contract(): pl.pallas_call(functools.partial(tiles_kernel, masks, halves), grid_spec=...  26 us
    ppermute x10, waiting for transfers between devices, grp_swap(): return lax.ppermute(a, 'grp', [(i, i ^ bits) for i in range(n_grp)])  18.5 us
    ppermute x10, starting transfers between devices, grp_swap(): return lax.ppermute(a, 'grp', [(i, i ^ bits) for i in range(n_grp)])  12.4 us
    ppermute x9, starting transfers between devices, blk_swap(): return lax.ppermute(a, 'blk', [(i, i ^ bits) for i in range(n_blk)])  10.6 us
    ppermute x9, waiting for transfers between devices, blk_swap(): return lax.ppermute(a, 'blk', [(i, i ^ bits) for i in range(n_blk)])  10.5 us
    reshape x3, local copies, waits for them, and re-layouts, local(): a_tiles.reshape(slots_here, PB, BS, BS).swapaxes(2, 3)  3.62 us
  transfers between devices with their start and end apart: 19, of which 10 were waited for; matrix products, arithmetic and copies ran while one was open for 6% of the time, Pallas kernels for 42%

profile of v2, /device:TPU:0, one launch (start us, length us, event | category | flops | bytes accessed | tf_op | source)
XLA Modules:
  0.0 130.3 jit_solution(339586301921594596)
XLA Ops:
  0.0 1.8 %reshape.158 = bf16[4,32,32,32]{3,2,1,0:T(8,128)(2,1)S(1)} reshape(bf16[4,32,1024]{2,1,0:T(8,128)(2,1)} %param.10) | data formatting | bytes 524288 | tf_op jit(solution)/shard_map/reshape | solution.py:227
  2.5 1.1 reshape.159
  3.6 3.1 %collective-permute-start = (bf16[4,32,1024]{2,1,0:T(8,128)(2,1)S(1)}, bf16[4,32,1024]{2,1,0:T(8,128)(2,1)S(1)}, u32[]{:S(2)}, u32[]{:S(2)}) collective-permute-start(bf16[4,32,1024]{2,1,0:T(8,128)(2,1)S(1)} %reshape.159), channel_id=1, source_target_pairs={{0,2},{1,3},{2,0},{3,1},{4,6},{5,7},{6,4},{7,5},{8,10},{9,11},{10,... | collective-permute-start | bytes 786440 | tf_op jit(solution)/shard_map/ppermute | solution.py:222
  6.8 2.6 %collective-permute-start.1 = (bf16[4,32,1024]{2,1,0:T(8,128)(2,1)S(1)}, bf16[4,32,1024]{2,1,0:T(8,128)(2,1)}, u32[]{:S(2)}, u32[]{:S(2)}) collective-permute-start(bf16[4,32,1024]{2,1,0:T(8,128)(2,1)S(1)} %reshape.159), channel_id=1, source_target_pairs={{0,4},{1,5},{2,6},{3,7},{4,0},{5,1},{6,2},{7,3},{8,12},{9,13},{10,... | collective-permute-start | bytes 786440 | tf_op jit(solution)/shard_map/ppermute | solution.py:222
  10.1 0.9 fusion.6
  12.2 7.5 %collective-permute-done.3 = bf16[1,496,48]{1,2,0:T(8,128)(2,1)S(1)} collective-permute-done((bf16[1,496,48]{1,2,0:T(8,128)(2,1)S(1)}, bf16[1,496,48]{1,2,0:T(8,128)(2,1)S(1)}, u32[]{:S(2)}, u32[]{:S(2)}) %collective-permute-start.3) | collective-permute-done | bytes 47648 | tf_op jit(solution)/shard_map/ppermute | solution.py:222
  19.6 3.0 %collective-permute-start.4 = (bf16[2,496,48]{1,2,0:T(8,128)(2,1)S(1)}, bf16[2,496,48]{1,2,0:T(8,128)(2,1)S(1)}, u32[]{:S(2)}, u32[]{:S(2)}) collective-permute-start(bf16[2,496,48]{1,2,0:T(8,128)(2,1)S(1)} %pad_maximum_fusion.5), channel_id=1, source_target_pairs={{0,4},{1,5},{2,6},{3,7},{4,0},{5,1},{6,2},{7,3},{8,12},{9,13},{10,... | collective-permute-start | bytes 285704 | tf_op jit(solution)/shard_map/ppermute | solution.py:222
  22.6 4.2 %collective-permute-done.4 = bf16[2,496,48]{1,2,0:T(8,128)(2,1)S(1)} collective-permute-done((bf16[2,496,48]{1,2,0:T(8,128)(2,1)S(1)}, bf16[2,496,48]{1,2,0:T(8,128)(2,1)S(1)}, u32[]{:S(2)}, u32[]{:S(2)}) %collective-permute-start.4) | collective-permute-done | bytes 95264 | tf_op jit(solution)/shard_map/ppermute | solution.py:222
  26.9 1.4 %collective-permute-done.5 = bf16[4,496,48]{1,2,0:T(8,128)(2,1)S(1)} collective-permute-done((bf16[4,496,48]{1,2,0:T(8,128)(2,1)S(1)}, bf16[4,496,48]{1,2,0:T(8,128)(2,1)S(1)}, u32[]{:S(2)}, u32[]{:S(2)}) %collective-permute-start.5) | collective-permute-done | bytes 190496 | tf_op jit(solution)/shard_map/ppermute | solution.py:222
  29.9 1.6 %collective-permute-start.6 = (bf16[112,96]{1,0:T(8,128)(2,1)S(1)}, bf16[112,96]{1,0:T(8,128)(2,1)S(1)}, u32[]{:S(2)}, u32[]{:S(2)}) collective-permute-start(bf16[112,96]{1,0:T(8,128)(2,1)S(1)} %get-tuple-element.37), channel_id=1, source_target_pairs={{0,8},{8,0},{16,24},{24,16},{1,9},{9,1},{17,25},{25,17},{2,10},{10... | collective-permute-start | bytes 64520 | tf_op jit(solution)/shard_map/ppermute | solution.py:225
  31.5 1.5 %collective-permute-start.7 = (bf16[112,96]{1,0:T(8,128)(2,1)S(1)}, bf16[112,96]{1,0:T(8,128)(2,1)S(1)}, u32[]{:S(2)}, u32[]{:S(2)}) collective-permute-start(bf16[112,96]{1,0:T(8,128)(2,1)S(1)} %get-tuple-element.38), channel_id=1, source_target_pairs={{0,16},{8,24},{16,0},{24,8},{1,17},{9,25},{17,1},{25,9},{2,18},{10... | collective-permute-start | bytes 64520 | tf_op jit(solution)/shard_map/ppermute | solution.py:225
  34.1 0.8 pad_maximum_fusion.1.gv_ref
  34.8 2.6 %collective-permute-start.2 = (bf16[4,32,1024]{2,1,0:T(8,128)(2,1)S(1)}, bf16[4,32,1024]{2,1,0:T(8,128)(2,1)S(1)}, u32[]{:S(2)}, u32[]{:S(2)}) collective-permute-start(bf16[4,32,1024]{2,1,0:T(8,128)(2,1)S(1)} %reshape.159), channel_id=1, source_target_pairs={{0,6},{1,7},{2,4},{3,5},{4,2},{5,3},{6,0},{7,1},{8,14},{9,15},{10,... | collective-permute-start | bytes 786440 | tf_op jit(solution)/shard_map/ppermute | solution.py:222
  39.2 10.4 %transform.3.refs_0_ = bf16[12,3,1024,256]{3,2,1,0:T(8,128)(2,1)} custom-call(bf16[3,384,96]{2,1,0:T(8,128)(2,1)} %pad_maximum_fusion.1.gv_ref, bf16[448,96]{1,0:T(8,128)(2,1)} %pad_maximum_fusion.4.go_ref, bf16[96,96,512]{2,1,0:T(8,128)(2,1)} %bitcast.51), custom_call_target="tpu_custom_call" | custom-call | flops 7500000256 | bytes 12582912 | tf_op jit(solution)/shard_map/transform/pallas_call | solution.py:68
  49.7 1.0 constant_dynamic-update-slice_fusion.1
  50.7 1.3 collective-permute-start.11
  52.0 1.5 %collective-permute-start.12 = (bf16[16,32,1024]{2,1,0:T(8,128)(2,1)S(1)}, bf16[16,32,1024]{2,1,0:T(8,128)(2,1)}, u32[]{:S(2)}, u32[]{:S(2)}) collective-permute-start(bf16[16,32,1024]{2,1,0:T(8,128)(2,1)S(1)} %constant_dynamic-update-slice_fusion.refs_0_), channel_id=1, source_target_pairs={{0,16},{8,24},{16,0},{24,8},{1,17},{9,25},{17,1},{25,9},{2,18},{10... | collective-permute-start | bytes 3145736 | tf_op jit(solution)/shard_map/ppermute | solution.py:225
  53.5 16.6 %transform.5.refs_7_.refs_3_ = bf16[12,3,1024,256]{3,2,1,0:T(8,128)(2,1)} custom-call(bf16[3,384,96]{2,1,0:T(8,128)(2,1)} %pad_maximum_fusion.1.gv_ref, bf16[448,96]{1,0:T(8,128)(2,1)} %pad_maximum_fusion.4.go_ref, bf16[96,96,512]{2,1,0:T(8,128)(2,1)} %bitcast.52), custom_call_target="tpu_custom_call" | custom-call | flops 15000000512 | bytes 12582912 | tf_op jit(solution)/shard_map/transform/pallas_call | solution.py:68
  70.1 10.7 %transform.4.refs_6_.refs_2_ = bf16[12,3,1024,256]{3,2,1,0:T(8,128)(2,1)} custom-call(bf16[3,384,96]{2,1,0:T(8,128)(2,1)} %pad_maximum_fusion.1.gv_ref, bf16[448,96]{1,0:T(8,128)(2,1)} %pad_maximum_fusion.4.go_ref, bf16[96,96,512]{2,1,0:T(8,128)(2,1)} %bitcast.53, bf16[12,3,1024,256]{3,2,1,0:T(8,128)(2,1)} %transform.3.refs_0_), custom_call_target="tpu_custom_call", output_to_operand_aliasing={{}: (3, {})} | custom-call | flops 7500000256 | bytes 12582912 | tf_op jit(solution)/shard_map/transform/pallas_call | solution.py:68
  81.4 0.8 collective-permute-start.9
  82.9 1.0 collective-permute-done.13.refs_3_
  83.9 1.5 %collective-permute-done.14.refs_5_ = bf16[16,32,1024]{2,1,0:T(8,128)(2,1)} collective-permute-done((bf16[16,32,1024]{2,1,0:T(8,128)(2,1)}, bf16[16,32,1024]{2,1,0:T(8,128)(2,1)}, u32[]{:S(2)}, u32[]{:S(2)}) %collective-permute-start.14) | collective-permute-done | bytes 1048608 | tf_op jit(solution)/shard_map/ppermute | solution.py:222
  85.4 17.2 %contract.2 = f32[17,32,512]{2,1,0:T(8,128)} custom-call(s32[128]{0:T(128)} %add.152.code_ref, bf16[16,32,1024]{2,1,0:T(8,128)(2,1)} %copy-done.3, bf16[16,32,1024]{2,1,0:T(8,128)(2,1)} %collective-permute-done.10.refs_1_, bf16[16,32,1024]{2,1,0:T(8,128)(2,1)} %collective-permute-done.11.refs_2_, bf16[16,32,1024]{2,1,0:T(8,128)(2,1)} %collective-permute-done.13.refs_3_, ...), custom_call_target="tpu_custom_call" | custom-call | flops 12000000000 | bytes 37748736 | tf_op jit(solution)/shard_map/contract/pallas_call | solution.py:181
  102.6 5.2 %collective-permute-done.9.refs_0_ = bf16[16,32,1024]{2,1,0:T(8,128)(2,1)} collective-permute-done((bf16[16,32,1024]{2,1,0:T(8,128)(2,1)S(1)}, bf16[16,32,1024]{2,1,0:T(8,128)(2,1)}, u32[]{:S(2)}, u32[]{:S(2)}) %collective-permute-start.9) | collective-permute-done | bytes 1048608 | tf_op jit(solution)/shard_map/ppermute | solution.py:225
  107.8 3.0 %collective-permute-done.15.refs_1_ = bf16[16,32,1024]{2,1,0:T(8,128)(2,1)} collective-permute-done((bf16[16,32,1024]{2,1,0:T(8,128)(2,1)}, bf16[16,32,1024]{2,1,0:T(8,128)(2,1)}, u32[]{:S(2)}, u32[]{:S(2)}) %collective-permute-start.15) | collective-permute-done | bytes 1048608 | tf_op jit(solution)/shard_map/ppermute | solution.py:222
  110.8 8.8 %contract.3 = f32[17,32,512]{2,1,0:T(8,128)} custom-call(s32[128]{0:T(128)} %add.152.code_ref, bf16[16,32,1024]{2,1,0:T(8,128)(2,1)} %collective-permute-done.9.refs_0_, bf16[16,32,1024]{2,1,0:T(8,128)(2,1)} %collective-permute-done.15.refs_1_, bf16[12,3,1024,256]{3,2,1,0:T(8,128)(2,1)} %transform.4.refs_6_.refs_2_, ...), custom_call_target="tpu_custom_call" | custom-call | flops 4000000000 | bytes 12582912 | tf_op jit(solution)/shard_map/contract/pallas_call | solution.py:181
  119.6 1.4 %add_convert_fusion.2 = (bf16[4,32,512]{2,1,0:T(8,128)(2,1)S(1)}, bf16[4,32,512]{2,1,0:T(8,128)(2,1)S(1)}, bf16[4,32,512]{2,1,0:T(8,128)(2,1)S(1)}, f32[4,32,512]{2,1,0:T(8,128)S(1)}) fusion(f32[17,32,512]{2,1,0:T(8,128)} %contract.3, s32[]{:T(128)S(6)} %select_n.125, f32[17,32,512]{2,1,0:T(8,128)S(1)} %copy-done.2, s32[]{:T(128)S(6)} %select_n.127, ...), kind=kLoop, calls=%fused_computation.12 | loop fusion | flops 458752 | bytes 2752528 | tf_op jit(solution)/shard_map/convert_element_type | solution.py:298
  121.1 0.7 collective-permute-start.17
  121.8 2.8 %collective-permute-start.18 = (bf16[128,512]{1,0:T(8,128)(2,1)S(1)}, bf16[128,512]{1,0:T(8,128)(2,1)S(1)}, u32[]{:S(2)}, u32[]{:S(2)}) collective-permute-start(bf16[128,512]{1,0:T(8,128)(2,1)S(1)} %bitcast.59), channel_id=1, source_target_pairs={{0,24},{8,16},{16,8},{24,0},{1,25},{9,17},{17,9},{25,1},{2,26},{10... | collective-permute-start | bytes 393224 | tf_op jit(solution)/shard_map/ppermute | solution.py:225
  124.6 2.9 %collective-permute-done.16 = bf16[128,512]{1,0:T(8,128)(2,1)S(1)} collective-permute-done((bf16[128,512]{1,0:T(8,128)(2,1)S(1)}, bf16[128,512]{1,0:T(8,128)(2,1)S(1)}, u32[]{:S(2)}, u32[]{:S(2)}) %collective-permute-start.16) | collective-permute-done | bytes 131104 | tf_op jit(solution)/shard_map/ppermute | solution.py:225
  127.4 2.1 %collective-permute-done.17 = bf16[128,512]{1,0:T(8,128)(2,1)S(1)} collective-permute-done((bf16[128,512]{1,0:T(8,128)(2,1)S(1)}, bf16[128,512]{1,0:T(8,128)(2,1)S(1)}, u32[]{:S(2)}, u32[]{:S(2)}) %collective-permute-start.17) | collective-permute-done | bytes 131104 | tf_op jit(solution)/shard_map/ppermute | solution.py:225
  129.5 0.8 fusion.1
  (88 shorter events, 8.5 us)
Async XLA Ops:
  0.0 11.5 %copy-start = (s32[12,12]{1,0:T(8,128)S(1)}, s32[12,12]{1,0:T(8,128)}, u32[]{:S(2)}) copy-start(s32[12,12]{1,0:T(8,128)} %param.9) | copy-start | bytes 1732
  3.6 46.0 %collective-permute-start = (bf16[4,32,1024]{2,1,0:T(8,128)(2,1)S(1)}, bf16[4,32,1024]{2,1,0:T(8,128)(2,1)S(1)}, u32[]{:S(2)}, u32[]{:S(2)}) collective-permute-start(bf16[4,32,1024]{2,1,0:T(8,128)(2,1)S(1)} %reshape.159), channel_id=1, source_target_pairs={{0,2},{1,3},{2,0},{3,1},{4,6},{5,7},{6,4},{7,5},{8,10},{9,11},{10,... | collective-permute-start | bytes 786440 | tf_op jit(solution)/shard_map/ppermute | solution.py:222
  6.8 42.9 %collective-permute-start.1 = (bf16[4,32,1024]{2,1,0:T(8,128)(2,1)S(1)}, bf16[4,32,1024]{2,1,0:T(8,128)(2,1)}, u32[]{:S(2)}, u32[]{:S(2)}) collective-permute-start(bf16[4,32,1024]{2,1,0:T(8,128)(2,1)S(1)} %reshape.159), channel_id=1, source_target_pairs={{0,4},{1,5},{2,6},{3,7},{4,0},{5,1},{6,2},{7,3},{8,12},{9,13},{10,... | collective-permute-start | bytes 786440 | tf_op jit(solution)/shard_map/ppermute | solution.py:222
  11.0 8.6 %collective-permute-start.3 = (bf16[1,496,48]{1,2,0:T(8,128)(2,1)S(1)}, bf16[1,496,48]{1,2,0:T(8,128)(2,1)S(1)}, u32[]{:S(2)}, u32[]{:S(2)}) collective-permute-start(bf16[1,496,48]{1,2,0:T(8,128)(2,1)S(1)} %fusion.6), channel_id=1, source_target_pairs={{0,2},{1,3},{2,0},{3,1},{4,6},{5,7},{6,4},{7,5},{8,10},{9,11},{10,... | collective-permute-start | bytes 142856 | tf_op jit(solution)/shard_map/ppermute | solution.py:222
  19.6 7.1 %collective-permute-start.4 = (bf16[2,496,48]{1,2,0:T(8,128)(2,1)S(1)}, bf16[2,496,48]{1,2,0:T(8,128)(2,1)S(1)}, u32[]{:S(2)}, u32[]{:S(2)}) collective-permute-start(bf16[2,496,48]{1,2,0:T(8,128)(2,1)S(1)} %pad_maximum_fusion.5), channel_id=1, source_target_pairs={{0,4},{1,5},{2,6},{3,7},{4,0},{5,1},{6,2},{7,3},{8,12},{9,13},{10,... | collective-permute-start | bytes 285704 | tf_op jit(solution)/shard_map/ppermute | solution.py:222
  26.8 1.5 %collective-permute-start.5 = (bf16[4,496,48]{1,2,0:T(8,128)(2,1)S(1)}, bf16[4,496,48]{1,2,0:T(8,128)(2,1)S(1)}, u32[]{:S(2)}, u32[]{:S(2)}) collective-permute-start(bf16[4,496,48]{1,2,0:T(8,128)(2,1)S(1)} %pad_maximum_fusion.2), channel_id=1, source_target_pairs={{0,1},{1,0},{2,3},{3,2},{4,5},{5,4},{6,7},{7,6},{8,9},{9,8},{10,11... | collective-permute-start | bytes 571400 | tf_op jit(solution)/shard_map/ppermute | solution.py:222
  29.9 4.9 %collective-permute-start.6 = (bf16[112,96]{1,0:T(8,128)(2,1)S(1)}, bf16[112,96]{1,0:T(8,128)(2,1)S(1)}, u32[]{:S(2)}, u32[]{:S(2)}) collective-permute-start(bf16[112,96]{1,0:T(8,128)(2,1)S(1)} %get-tuple-element.37), channel_id=1, source_target_pairs={{0,8},{8,0},{16,24},{24,16},{1,9},{9,1},{17,25},{25,17},{2,10},{10... | collective-permute-start | bytes 64520 | tf_op jit(solution)/shard_map/ppermute | solution.py:225
  31.5 6.0 %collective-permute-start.7 = (bf16[112,96]{1,0:T(8,128)(2,1)S(1)}, bf16[112,96]{1,0:T(8,128)(2,1)S(1)}, u32[]{:S(2)}, u32[]{:S(2)}) collective-permute-start(bf16[112,96]{1,0:T(8,128)(2,1)S(1)} %get-tuple-element.38), channel_id=1, source_target_pairs={{0,16},{8,24},{16,0},{24,8},{1,17},{9,25},{17,1},{25,9},{2,18},{10... | collective-permute-start | bytes 64520 | tf_op jit(solution)/shard_map/ppermute | solution.py:225
  33.0 4.8 %collective-permute-start.8 = (bf16[112,96]{1,0:T(8,128)(2,1)S(1)}, bf16[112,96]{1,0:T(8,128)(2,1)S(1)}, u32[]{:S(2)}, u32[]{:S(2)}) collective-permute-start(bf16[112,96]{1,0:T(8,128)(2,1)S(1)} %get-tuple-element.39), channel_id=1, source_target_pairs={{0,24},{8,16},{16,8},{24,0},{1,25},{9,17},{17,9},{25,1},{2,26},{10... | collective-permute-start | bytes 64520 | tf_op jit(solution)/shard_map/ppermute | solution.py:225
  34.8 14.8 %collective-permute-start.2 = (bf16[4,32,1024]{2,1,0:T(8,128)(2,1)S(1)}, bf16[4,32,1024]{2,1,0:T(8,128)(2,1)S(1)}, u32[]{:S(2)}, u32[]{:S(2)}) collective-permute-start(bf16[4,32,1024]{2,1,0:T(8,128)(2,1)S(1)} %reshape.159), channel_id=1, source_target_pairs={{0,6},{1,7},{2,4},{3,5},{4,2},{5,3},{6,0},{7,1},{8,14},{9,15},{10,... | collective-permute-start | bytes 786440 | tf_op jit(solution)/shard_map/ppermute | solution.py:222
  37.5 1.8 %copy-start.4 = (bf16[112,96]{1,0:T(8,128)(2,1)}, bf16[112,96]{1,0:T(8,128)(2,1)S(1)}, u32[]{:S(2)}) copy-start(bf16[112,96]{1,0:T(8,128)(2,1)S(1)} %collective-permute-done.7) | copy-start | bytes 64516
  37.8 1.4 %copy-start.6 = (bf16[112,96]{1,0:T(8,128)(2,1)}, bf16[112,96]{1,0:T(8,128)(2,1)S(1)}, u32[]{:S(2)}) copy-start(bf16[112,96]{1,0:T(8,128)(2,1)S(1)} %collective-permute-done.8) | copy-start | bytes 64516
  50.7 30.7 %copy-start.3 = (bf16[16,32,1024]{2,1,0:T(8,128)(2,1)}, bf16[16,32,1024]{2,1,0:T(8,128)(2,1)S(1)}, u32[]{:S(2)}) copy-start(bf16[16,32,1024]{2,1,0:T(8,128)(2,1)S(1)} %constant_dynamic-update-slice_fusion.refs_0_) | copy-start | bytes 3145732
  50.7 30.1 %collective-permute-start.11 = (bf16[16,32,1024]{2,1,0:T(8,128)(2,1)S(1)}, bf16[16,32,1024]{2,1,0:T(8,128)(2,1)}, u32[]{:S(2)}, u32[]{:S(2)}) collective-permute-start(bf16[16,32,1024]{2,1,0:T(8,128)(2,1)S(1)} %constant_dynamic-update-slice_fusion.refs_0_), channel_id=1, source_target_pairs={{0,8},{8,0},{16,24},{24,16},{1,9},{9,1},{17,25},{25,17},{2,10},{10... | collective-permute-start | bytes 3145736 | tf_op jit(solution)/shard_map/ppermute | solution.py:225
  52.0 28.9 %collective-permute-start.12 = (bf16[16,32,1024]{2,1,0:T(8,128)(2,1)S(1)}, bf16[16,32,1024]{2,1,0:T(8,128)(2,1)}, u32[]{:S(2)}, u32[]{:S(2)}) collective-permute-start(bf16[16,32,1024]{2,1,0:T(8,128)(2,1)S(1)} %constant_dynamic-update-slice_fusion.refs_0_), channel_id=1, source_target_pairs={{0,16},{8,24},{16,0},{24,8},{1,17},{9,25},{17,1},{25,9},{2,18},{10... | collective-permute-start | bytes 3145736 | tf_op jit(solution)/shard_map/ppermute | solution.py:225
  70.1 12.1 %copy-start.5 = (bf16[112,96]{1,0:T(8,128)(2,1)S(1)}, bf16[112,96]{1,0:T(8,128)(2,1)}, u32[]{:S(2)}) copy-start(bf16[112,96]{1,0:T(8,128)(2,1)} %copy-done.4) | copy-start | bytes 64516
  70.1 12.1 %copy-start.7 = (bf16[112,96]{1,0:T(8,128)(2,1)S(1)}, bf16[112,96]{1,0:T(8,128)(2,1)}, u32[]{:S(2)}) copy-start(bf16[112,96]{1,0:T(8,128)(2,1)} %copy-done.6) | copy-start | bytes 64516
  70.1 12.8 %collective-permute-start.10 = (bf16[16,32,1024]{2,1,0:T(8,128)(2,1)S(1)}, bf16[16,32,1024]{2,1,0:T(8,128)(2,1)}, u32[]{:S(2)}, u32[]{:S(2)}) collective-permute-start(bf16[16,32,1024]{2,1,0:T(8,128)(2,1)S(1)} %constant_dynamic-update-slice_fusion.refs_0_), channel_id=1, source_target_pairs={{0,1},{1,0},{2,3},{3,2},{4,5},{5,4},{6,7},{7,6},{8,9},{9,8},{10,11... | collective-permute-start | bytes 3145736 | tf_op jit(solution)/shard_map/ppermute | solution.py:222
  80.8 3.1 %collective-permute-start.13 = (bf16[16,32,1024]{2,1,0:T(8,128)(2,1)}, bf16[16,32,1024]{2,1,0:T(8,128)(2,1)}, u32[]{:S(2)}, u32[]{:S(2)}) collective-permute-start(bf16[16,32,1024]{2,1,0:T(8,128)(2,1)} %collective-permute-done.11.refs_2_), channel_id=1, source_target_pairs={{0,1},{1,0},{2,3},{3,2},{4,5},{5,4},{6,7},{7,6},{8,9},{9,8},{10,11... | collective-permute-start | bytes 3145736 | tf_op jit(solution)/shard_map/ppermute | solution.py:222
  81.2 4.2 %collective-permute-start.14 = (bf16[16,32,1024]{2,1,0:T(8,128)(2,1)}, bf16[16,32,1024]{2,1,0:T(8,128)(2,1)}, u32[]{:S(2)}, u32[]{:S(2)}) collective-permute-start(bf16[16,32,1024]{2,1,0:T(8,128)(2,1)} %collective-permute-done.12.refs_4_), channel_id=1, source_target_pairs={{0,1},{1,0},{2,3},{3,2},{4,5},{5,4},{6,7},{7,6},{8,9},{9,8},{10,11... | collective-permute-start | bytes 3145736 | tf_op jit(solution)/shard_map/ppermute | solution.py:222
  81.4 26.4 %collective-permute-start.9 = (bf16[16,32,1024]{2,1,0:T(8,128)(2,1)S(1)}, bf16[16,32,1024]{2,1,0:T(8,128)(2,1)}, u32[]{:S(2)}, u32[]{:S(2)}) collective-permute-start(bf16[16,32,1024]{2,1,0:T(8,128)(2,1)S(1)} %constant_dynamic-update-slice_fusion.refs_0_), channel_id=1, source_target_pairs={{0,24},{8,16},{16,8},{24,0},{1,25},{9,17},{17,9},{25,1},{2,26},{10... | collective-permute-start | bytes 3145736 | tf_op jit(solution)/shard_map/ppermute | solution.py:225
  107.8 3.0 %collective-permute-start.15 = (bf16[16,32,1024]{2,1,0:T(8,128)(2,1)}, bf16[16,32,1024]{2,1,0:T(8,128)(2,1)}, u32[]{:S(2)}, u32[]{:S(2)}) collective-permute-start(bf16[16,32,1024]{2,1,0:T(8,128)(2,1)} %collective-permute-done.9.refs_0_), channel_id=1, source_target_pairs={{0,1},{1,0},{2,3},{3,2},{4,5},{5,4},{6,7},{7,6},{8,9},{9,8},{10,11... | collective-permute-start | bytes 3145736 | tf_op jit(solution)/shard_map/ppermute | solution.py:222
  107.8 11.8 %copy-start.2 = (f32[17,32,512]{2,1,0:T(8,128)S(1)}, f32[17,32,512]{2,1,0:T(8,128)}, u32[]{:S(2)}) copy-start(f32[17,32,512]{2,1,0:T(8,128)} %contract.2) | copy-start | bytes 3342340
  110.8 19.5 %copy-start.1 = (s32[12,12]{1,0:T(8,128)S(1)}, s32[12,12]{1,0:T(8,128)}, u32[]{:S(2)}) copy-start(s32[12,12]{1,0:T(8,128)} %param.9) | copy-start | bytes 1732
  121.0 6.4 %collective-permute-start.16 = (bf16[128,512]{1,0:T(8,128)(2,1)S(1)}, bf16[128,512]{1,0:T(8,128)(2,1)S(1)}, u32[]{:S(2)}, u32[]{:S(2)}) collective-permute-start(bf16[128,512]{1,0:T(8,128)(2,1)S(1)} %bitcast.61), channel_id=1, source_target_pairs={{0,8},{8,0},{16,24},{24,16},{1,9},{9,1},{17,25},{25,17},{2,10},{10... | collective-permute-start | bytes 393224 | tf_op jit(solution)/shard_map/ppermute | solution.py:225
  121.1 8.4 %collective-permute-start.17 = (bf16[128,512]{1,0:T(8,128)(2,1)S(1)}, bf16[128,512]{1,0:T(8,128)(2,1)S(1)}, u32[]{:S(2)}, u32[]{:S(2)}) collective-permute-start(bf16[128,512]{1,0:T(8,128)(2,1)S(1)} %bitcast.60), channel_id=1, source_target_pairs={{0,16},{8,24},{16,0},{24,8},{1,17},{9,25},{17,1},{25,9},{2,18},{10... | collective-permute-start | bytes 393224 | tf_op jit(solution)/shard_map/ppermute | solution.py:225
  121.8 7.7 %collective-permute-start.18 = (bf16[128,512]{1,0:T(8,128)(2,1)S(1)}, bf16[128,512]{1,0:T(8,128)(2,1)S(1)}, u32[]{:S(2)}, u32[]{:S(2)}) collective-permute-start(bf16[128,512]{1,0:T(8,128)(2,1)S(1)} %bitcast.59), channel_id=1, source_target_pairs={{0,24},{8,16},{16,8},{24,0},{1,25},{9,17},{17,9},{25,1},{2,26},{10... | collective-permute-start | bytes 393224 | tf_op jit(solution)/shard_map/ppermute | solution.py:225

commit v3 on v2

--- a/solution.py
+++ b/solution.py
@@ -277,12 +277,14 @@
     for h in range(1, q // cols):
         paired.append(transform(b, virt, occ, cols, h, 0, blocks // NU_PART))
     sums = []
-    for at in range(0, n_blk, 3):
-        masks = range(at, min(at + 3, n_blk))
+    for at in range(0, n_blk, 2):
+        masks = range(at, at + 2)
         mine = [near[m] for m in masks]
         if sums:
-            mine, sums[-1] = lax.optimization_barrier((mine, sums[-1]))
             far = []
+            for i, tiles in enumerate(mine):
+                mine[i], sums[-1], far = lax.optimization_barrier((tiles, sums[-1], far))
+                far.append(grp_swap(mine[i], 1))
         else:
             far = [grp_swap(mine[0], 1)]
             mine[1:], paired = lax.optimization_barrier((mine[1:], paired))

time: 131 us -> 158 us (1.21)
  waiting for transfers between devices: 28.9 us -> 57.3 us
    ppermute x9, waiting for transfers between devices: 10.5 us -> 38.4 us  [blk_swap(): return lax.ppermute(a, 'blk', [(i, i ^ bits) for i in range(n_blk)])]
  transfers between devices with their start and end apart: 19 -> 19, of which waited for: 10 -> 10; matrix products, arithmetic and copies ran while one was open for 6% -> 5% of each run, Pallas kernels for 42% -> 32%
where the time goes in v3:
time: 158 us
  Pallas kernels  63 us (40%)
  waiting for transfers between devices  57.3 us (36%)
  starting transfers between devices  22.9 us (14%)
  local copies, waits for them, and re-layouts  8.29 us (5%)
  other arithmetic  5.93 us (4%)
    ppermute x9, waiting for transfers between devices, blk_swap(): return lax.ppermute(a, 'blk', [(i, i ^ bits) for i in range(n_blk)])  38.4 us
    pallas_call x3, Pallas kernels, transform(): pl.pallas_call(functools.partial(transform_kernel, pitch, begin), grid=(e...  37.8 us
    pallas_call x2, Pallas kernels, contract(): pl.pallas_call(functools.partial(tiles_kernel, masks, halves), grid_spec=...  25.2 us
    ppermute x10, waiting for transfers between devices, grp_swap(): return lax.ppermute(a, 'grp', [(i, i ^ bits) for i in range(n_grp)])  18.9 us
    ppermute x10, starting transfers between devices, grp_swap(): return lax.ppermute(a, 'grp', [(i, i ^ bits) for i in range(n_grp)])  12.2 us
    ppermute x9, starting transfers between devices, blk_swap(): return lax.ppermute(a, 'blk', [(i, i ^ bits) for i in range(n_blk)])  10.7 us
    reshape x3, local copies, waits for them, and re-layouts, local(): a_tiles.reshape(slots_here, PB, BS, BS).swapaxes(2, 3)  3.62 us
  transfers between devices with their start and end apart: 19, of which 10 were waited for; matrix products, arithmetic and copies ran while one was open for 5% of the time, Pallas kernels for 32%

profile of v3, /device:TPU:0, one launch (start us, length us, event | category | flops | bytes accessed | tf_op | source)
XLA Modules:
  0.0 157.7 jit_solution(486931724963001581)
XLA Ops:
  0.0 1.8 %reshape.158 = bf16[4,32,32,32]{3,2,1,0:T(8,128)(2,1)S(1)} reshape(bf16[4,32,1024]{2,1,0:T(8,128)(2,1)} %param.10) | data formatting | bytes 524288 | tf_op jit(solution)/shard_map/reshape | solution.py:227
  2.5 1.1 reshape.159
  3.6 3.1 %collective-permute-start = (bf16[4,32,1024]{2,1,0:T(8,128)(2,1)S(1)}, bf16[4,32,1024]{2,1,0:T(8,128)(2,1)S(1)}, u32[]{:S(2)}, u32[]{:S(2)}) collective-permute-start(bf16[4,32,1024]{2,1,0:T(8,128)(2,1)S(1)} %reshape.159), channel_id=1, source_target_pairs={{0,2},{1,3},{2,0},{3,1},{4,6},{5,7},{6,4},{7,5},{8,10},{9,11},{10,... | collective-permute-start | bytes 786440 | tf_op jit(solution)/shard_map/ppermute | solution.py:222
  6.8 2.6 %collective-permute-start.1 = (bf16[4,32,1024]{2,1,0:T(8,128)(2,1)S(1)}, bf16[4,32,1024]{2,1,0:T(8,128)(2,1)}, u32[]{:S(2)}, u32[]{:S(2)}) collective-permute-start(bf16[4,32,1024]{2,1,0:T(8,128)(2,1)S(1)} %reshape.159), channel_id=1, source_target_pairs={{0,4},{1,5},{2,6},{3,7},{4,0},{5,1},{6,2},{7,3},{8,12},{9,13},{10,... | collective-permute-start | bytes 786440 | tf_op jit(solution)/shard_map/ppermute | solution.py:222
  10.1 0.9 fusion.6
  12.2 7.5 %collective-permute-done.3 = bf16[1,496,48]{1,2,0:T(8,128)(2,1)S(1)} collective-permute-done((bf16[1,496,48]{1,2,0:T(8,128)(2,1)S(1)}, bf16[1,496,48]{1,2,0:T(8,128)(2,1)S(1)}, u32[]{:S(2)}, u32[]{:S(2)}) %collective-permute-start.3) | collective-permute-done | bytes 47648 | tf_op jit(solution)/shard_map/ppermute | solution.py:222
  19.6 3.0 %collective-permute-start.4 = (bf16[2,496,48]{1,2,0:T(8,128)(2,1)S(1)}, bf16[2,496,48]{1,2,0:T(8,128)(2,1)S(1)}, u32[]{:S(2)}, u32[]{:S(2)}) collective-permute-start(bf16[2,496,48]{1,2,0:T(8,128)(2,1)S(1)} %pad_maximum_fusion.5), channel_id=1, source_target_pairs={{0,4},{1,5},{2,6},{3,7},{4,0},{5,1},{6,2},{7,3},{8,12},{9,13},{10,... | collective-permute-start | bytes 285704 | tf_op jit(solution)/shard_map/ppermute | solution.py:222
  22.6 4.2 %collective-permute-done.4 = bf16[2,496,48]{1,2,0:T(8,128)(2,1)S(1)} collective-permute-done((bf16[2,496,48]{1,2,0:T(8,128)(2,1)S(1)}, bf16[2,496,48]{1,2,0:T(8,128)(2,1)S(1)}, u32[]{:S(2)}, u32[]{:S(2)}) %collective-permute-start.4) | collective-permute-done | bytes 95264 | tf_op jit(solution)/shard_map/ppermute | solution.py:222
  26.9 1.4 collective-permute-done.5
  29.9 1.6 collective-permute-start.6
  31.5 1.5 collective-permute-start.7
  34.1 0.8 pad_maximum_fusion.1.gv_ref
  34.8 2.6 %collective-permute-start.2 = (bf16[4,32,1024]{2,1,0:T(8,128)(2,1)S(1)}, bf16[4,32,1024]{2,1,0:T(8,128)(2,1)S(1)}, u32[]{:S(2)}, u32[]{:S(2)}) collective-permute-start(bf16[4,32,1024]{2,1,0:T(8,128)(2,1)S(1)} %reshape.159), channel_id=1, source_target_pairs={{0,6},{1,7},{2,4},{3,5},{4,2},{5,3},{6,0},{7,1},{8,14},{9,15},{10,... | collective-permute-start | bytes 786440 | tf_op jit(solution)/shard_map/ppermute | solution.py:222
  39.2 10.4 %transform.3.refs_0_ = bf16[12,3,1024,256]{3,2,1,0:T(8,128)(2,1)} custom-call(bf16[3,384,96]{2,1,0:T(8,128)(2,1)} %pad_maximum_fusion.1.gv_ref, bf16[448,96]{1,0:T(8,128)(2,1)} %pad_maximum_fusion.4.go_ref, bf16[96,96,512]{2,1,0:T(8,128)(2,1)} %bitcast.51), custom_call_target="tpu_custom_call" | custom-call | flops 7500000256 | bytes 12582912 | tf_op jit(solution)/shard_map/transform/pallas_call | solution.py:68
  49.7 1.0 constant_dynamic-update-slice_fusion.1
  50.7 1.3 collective-permute-start.12
  52.0 16.8 %transform.5.refs_5_ = bf16[12,3,1024,256]{3,2,1,0:T(8,128)(2,1)} custom-call(bf16[3,384,96]{2,1,0:T(8,128)(2,1)} %pad_maximum_fusion.1.gv_ref, bf16[448,96]{1,0:T(8,128)(2,1)} %pad_maximum_fusion.4.go_ref, bf16[96,96,512]{2,1,0:T(8,128)(2,1)} %bitcast.52), custom_call_target="tpu_custom_call" | custom-call | flops 15000000512 | bytes 12582912 | tf_op jit(solution)/shard_map/transform/pallas_call | solution.py:68
  68.8 10.6 %transform.4.refs_4_ = bf16[12,3,1024,256]{3,2,1,0:T(8,128)(2,1)} custom-call(bf16[3,384,96]{2,1,0:T(8,128)(2,1)} %pad_maximum_fusion.1.gv_ref, bf16[448,96]{1,0:T(8,128)(2,1)} %pad_maximum_fusion.4.go_ref, bf16[96,96,512]{2,1,0:T(8,128)(2,1)} %bitcast.53, bf16[12,3,1024,256]{3,2,1,0:T(8,128)(2,1)} %transform.3.refs_0_), custom_call_target="tpu_custom_call", output_to_operand_aliasing={{}: (3, {})} | custom-call | flops 7500000256 | bytes 12582912 | tf_op jit(solution)/shard_map/transform/pallas_call | solution.py:68
  79.7 1.5 collective-permute-start.10
  81.2 0.8 collective-permute-start.9
  82.7 12.5 %contract.2 = f32[17,32,512]{2,1,0:T(8,128)} custom-call(s32[128]{0:T(128)} %add.152.code_ref, bf16[16,32,1024]{2,1,0:T(8,128)(2,1)} %copy-done.3, bf16[16,32,1024]{2,1,0:T(8,128)(2,1)} %collective-permute-done.11.refs_1_, bf16[16,32,1024]{2,1,0:T(8,128)(2,1)} %collective-permute-done.12.refs_2_, bf16[16,32,1024]{2,1,0:T(8,128)(2,1)} %collective-permute-done.13.refs_3_, ...), custom_call_target="tpu_custom_call" | custom-call | flops 8000000000 | bytes 25165824 | tf_op jit(solution)/shard_map/contract/pallas_call | solution.py:181
  95.2 32.3 %collective-permute-done.10.refs_0_ = bf16[16,32,1024]{2,1,0:T(8,128)(2,1)} collective-permute-done((bf16[16,32,1024]{2,1,0:T(8,128)(2,1)S(1)}, bf16[16,32,1024]{2,1,0:T(8,128)(2,1)}, u32[]{:S(2)}, u32[]{:S(2)}) %collective-permute-start.10) | collective-permute-done | bytes 1048608 | tf_op jit(solution)/shard_map/ppermute | solution.py:225
  127.5 3.0 %collective-permute-done.14.refs_1_ = bf16[16,32,1024]{2,1,0:T(8,128)(2,1)} collective-permute-done((bf16[16,32,1024]{2,1,0:T(8,128)(2,1)}, bf16[16,32,1024]{2,1,0:T(8,128)(2,1)}, u32[]{:S(2)}, u32[]{:S(2)}) %collective-permute-start.14) | collective-permute-done | bytes 1048608 | tf_op jit(solution)/shard_map/ppermute | solution.py:222
  130.7 2.9 %collective-permute-done.15.refs_3_ = bf16[16,32,1024]{2,1,0:T(8,128)(2,1)} collective-permute-done((bf16[16,32,1024]{2,1,0:T(8,128)(2,1)}, bf16[16,32,1024]{2,1,0:T(8,128)(2,1)}, u32[]{:S(2)}, u32[]{:S(2)}) %collective-permute-start.15) | collective-permute-done | bytes 1048608 | tf_op jit(solution)/shard_map/ppermute | solution.py:222
  133.5 12.7 %contract.3 = f32[17,32,512]{2,1,0:T(8,128)} custom-call(s32[128]{0:T(128)} %add.152.code_ref, bf16[16,32,1024]{2,1,0:T(8,128)(2,1)} %collective-permute-done.10.refs_0_, bf16[16,32,1024]{2,1,0:T(8,128)(2,1)} %collective-permute-done.14.refs_1_, bf16[16,32,1024]{2,1,0:T(8,128)(2,1)} %collective-permute-done.9.refs_2_, ...), custom_call_target="tpu_custom_call" | custom-call | flops 8000000000 | bytes 25165824 | tf_op jit(solution)/shard_map/contract/pallas_call | solution.py:181
  146.2 1.4 add_convert_fusion.2
  147.6 0.9 collective-permute-start.16
  148.5 1.2 collective-permute-start.17
  149.7 1.4 collective-permute-start.18
  151.2 2.9 %collective-permute-done.16 = bf16[128,512]{1,0:T(8,128)(2,1)S(1)} collective-permute-done((bf16[128,512]{1,0:T(8,128)(2,1)S(1)}, bf16[128,512]{1,0:T(8,128)(2,1)S(1)}, u32[]{:S(2)}, u32[]{:S(2)}) %collective-permute-start.16) | collective-permute-done | bytes 131104 | tf_op jit(solution)/shard_map/ppermute | solution.py:225
  154.0 1.3 collective-permute-done.17
  155.3 1.6 %collective-permute-done.18 = bf16[128,512]{1,0:T(8,128)(2,1)S(1)} collective-permute-done((bf16[128,512]{1,0:T(8,128)(2,1)S(1)}, bf16[128,512]{1,0:T(8,128)(2,1)S(1)}, u32[]{:S(2)}, u32[]{:S(2)}) %collective-permute-start.18) | collective-permute-done | bytes 131104 | tf_op jit(solution)/shard_map/ppermute | solution.py:225
  (88 shorter events, 9.0 us)
Async XLA Ops:
  0.0 11.5 %copy-start = (s32[12,12]{1,0:T(8,128)S(1)}, s32[12,12]{1,0:T(8,128)}, u32[]{:S(2)}) copy-start(s32[12,12]{1,0:T(8,128)} %param.9) | copy-start | bytes 1732
  3.6 46.0 %collective-permute-start = (bf16[4,32,1024]{2,1,0:T(8,128)(2,1)S(1)}, bf16[4,32,1024]{2,1,0:T(8,128)(2,1)S(1)}, u32[]{:S(2)}, u32[]{:S(2)}) collective-permute-start(bf16[4,32,1024]{2,1,0:T(8,128)(2,1)S(1)} %reshape.159), channel_id=1, source_target_pairs={{0,2},{1,3},{2,0},{3,1},{4,6},{5,7},{6,4},{7,5},{8,10},{9,11},{10,... | collective-permute-start | bytes 786440 | tf_op jit(solution)/shard_map/ppermute | solution.py:222
  6.8 42.9 %collective-permute-start.1 = (bf16[4,32,1024]{2,1,0:T(8,128)(2,1)S(1)}, bf16[4,32,1024]{2,1,0:T(8,128)(2,1)}, u32[]{:S(2)}, u32[]{:S(2)}) collective-permute-start(bf16[4,32,1024]{2,1,0:T(8,128)(2,1)S(1)} %reshape.159), channel_id=1, source_target_pairs={{0,4},{1,5},{2,6},{3,7},{4,0},{5,1},{6,2},{7,3},{8,12},{9,13},{10,... | collective-permute-start | bytes 786440 | tf_op jit(solution)/shard_map/ppermute | solution.py:222
  11.0 8.6 %collective-permute-start.3 = (bf16[1,496,48]{1,2,0:T(8,128)(2,1)S(1)}, bf16[1,496,48]{1,2,0:T(8,128)(2,1)S(1)}, u32[]{:S(2)}, u32[]{:S(2)}) collective-permute-start(bf16[1,496,48]{1,2,0:T(8,128)(2,1)S(1)} %fusion.6), channel_id=1, source_target_pairs={{0,2},{1,3},{2,0},{3,1},{4,6},{5,7},{6,4},{7,5},{8,10},{9,11},{10,... | collective-permute-start | bytes 142856 | tf_op jit(solution)/shard_map/ppermute | solution.py:222
  19.6 7.1 %collective-permute-start.4 = (bf16[2,496,48]{1,2,0:T(8,128)(2,1)S(1)}, bf16[2,496,48]{1,2,0:T(8,128)(2,1)S(1)}, u32[]{:S(2)}, u32[]{:S(2)}) collective-permute-start(bf16[2,496,48]{1,2,0:T(8,128)(2,1)S(1)} %pad_maximum_fusion.5), channel_id=1, source_target_pairs={{0,4},{1,5},{2,6},{3,7},{4,0},{5,1},{6,2},{7,3},{8,12},{9,13},{10,... | collective-permute-start | bytes 285704 | tf_op jit(solution)/shard_map/ppermute | solution.py:222
  26.8 1.5 collective-permute-start.5
  29.9 4.9 %collective-permute-start.6 = (bf16[112,96]{1,0:T(8,128)(2,1)S(1)}, bf16[112,96]{1,0:T(8,128)(2,1)S(1)}, u32[]{:S(2)}, u32[]{:S(2)}) collective-permute-start(bf16[112,96]{1,0:T(8,128)(2,1)S(1)} %get-tuple-element.41), channel_id=1, source_target_pairs={{0,8},{8,0},{16,24},{24,16},{1,9},{9,1},{17,25},{25,17},{2,10},{10... | collective-permute-start | bytes 64520 | tf_op jit(solution)/shard_map/ppermute | solution.py:225
  31.5 6.0 %collective-permute-start.7 = (bf16[112,96]{1,0:T(8,128)(2,1)S(1)}, bf16[112,96]{1,0:T(8,128)(2,1)S(1)}, u32[]{:S(2)}, u32[]{:S(2)}) collective-permute-start(bf16[112,96]{1,0:T(8,128)(2,1)S(1)} %get-tuple-element.42), channel_id=1, source_target_pairs={{0,16},{8,24},{16,0},{24,8},{1,17},{9,25},{17,1},{25,9},{2,18},{10... | collective-permute-start | bytes 64520 | tf_op jit(solution)/shard_map/ppermute | solution.py:225
  33.0 4.8 %collective-permute-start.8 = (bf16[112,96]{1,0:T(8,128)(2,1)S(1)}, bf16[112,96]{1,0:T(8,128)(2,1)S(1)}, u32[]{:S(2)}, u32[]{:S(2)}) collective-permute-start(bf16[112,96]{1,0:T(8,128)(2,1)S(1)} %get-tuple-element.43), channel_id=1, source_target_pairs={{0,24},{8,16},{16,8},{24,0},{1,25},{9,17},{17,9},{25,1},{2,26},{10... | collective-permute-start | bytes 64520 | tf_op jit(solution)/shard_map/ppermute | solution.py:225
  34.8 14.8 %collective-permute-start.2 = (bf16[4,32,1024]{2,1,0:T(8,128)(2,1)S(1)}, bf16[4,32,1024]{2,1,0:T(8,128)(2,1)S(1)}, u32[]{:S(2)}, u32[]{:S(2)}) collective-permute-start(bf16[4,32,1024]{2,1,0:T(8,128)(2,1)S(1)} %reshape.159), channel_id=1, source_target_pairs={{0,6},{1,7},{2,4},{3,5},{4,2},{5,3},{6,0},{7,1},{8,14},{9,15},{10,... | collective-permute-start | bytes 786440 | tf_op jit(solution)/shard_map/ppermute | solution.py:222
  37.5 1.8 %copy-start.4 = (bf16[112,96]{1,0:T(8,128)(2,1)}, bf16[112,96]{1,0:T(8,128)(2,1)S(1)}, u32[]{:S(2)}) copy-start(bf16[112,96]{1,0:T(8,128)(2,1)S(1)} %collective-permute-done.7) | copy-start | bytes 64516
  37.8 1.4 copy-start.6
  50.7 30.5 %copy-start.3 = (bf16[16,32,1024]{2,1,0:T(8,128)(2,1)}, bf16[16,32,1024]{2,1,0:T(8,128)(2,1)S(1)}, u32[]{:S(2)}) copy-start(bf16[16,32,1024]{2,1,0:T(8,128)(2,1)S(1)} %constant_dynamic-update-slice_fusion.refs_0_) | copy-start | bytes 3145732
  50.7 28.7 %collective-permute-start.12 = (bf16[16,32,1024]{2,1,0:T(8,128)(2,1)S(1)}, bf16[16,32,1024]{2,1,0:T(8,128)(2,1)}, u32[]{:S(2)}, u32[]{:S(2)}) collective-permute-start(bf16[16,32,1024]{2,1,0:T(8,128)(2,1)S(1)} %constant_dynamic-update-slice_fusion.refs_0_), channel_id=1, source_target_pairs={{0,8},{8,0},{16,24},{24,16},{1,9},{9,1},{17,25},{25,17},{2,10},{10... | collective-permute-start | bytes 3145736 | tf_op jit(solution)/shard_map/ppermute | solution.py:225
  68.7 13.2 %copy-start.5 = (bf16[112,96]{1,0:T(8,128)(2,1)S(1)}, bf16[112,96]{1,0:T(8,128)(2,1)}, u32[]{:S(2)}) copy-start(bf16[112,96]{1,0:T(8,128)(2,1)} %copy-done.4) | copy-start | bytes 64516
  68.7 13.2 %copy-start.7 = (bf16[112,96]{1,0:T(8,128)(2,1)S(1)}, bf16[112,96]{1,0:T(8,128)(2,1)}, u32[]{:S(2)}) copy-start(bf16[112,96]{1,0:T(8,128)(2,1)} %copy-done.6) | copy-start | bytes 64516
  68.7 13.9 %collective-permute-start.11 = (bf16[16,32,1024]{2,1,0:T(8,128)(2,1)S(1)}, bf16[16,32,1024]{2,1,0:T(8,128)(2,1)}, u32[]{:S(2)}, u32[]{:S(2)}) collective-permute-start(bf16[16,32,1024]{2,1,0:T(8,128)(2,1)S(1)} %constant_dynamic-update-slice_fusion.refs_0_), channel_id=1, source_target_pairs={{0,1},{1,0},{2,3},{3,2},{4,5},{5,4},{6,7},{7,6},{8,9},{9,8},{10,11... | collective-permute-start | bytes 3145736 | tf_op jit(solution)/shard_map/ppermute | solution.py:222
  79.4 3.3 %collective-permute-start.13 = (bf16[16,32,1024]{2,1,0:T(8,128)(2,1)}, bf16[16,32,1024]{2,1,0:T(8,128)(2,1)}, u32[]{:S(2)}, u32[]{:S(2)}) collective-permute-start(bf16[16,32,1024]{2,1,0:T(8,128)(2,1)} %collective-permute-done.12.refs_2_), channel_id=1, source_target_pairs={{0,1},{1,0},{2,3},{3,2},{4,5},{5,4},{6,7},{7,6},{8,9},{9,8},{10,11... | collective-permute-start | bytes 3145736 | tf_op jit(solution)/shard_map/ppermute | solution.py:222
  79.7 47.9 %collective-permute-start.10 = (bf16[16,32,1024]{2,1,0:T(8,128)(2,1)S(1)}, bf16[16,32,1024]{2,1,0:T(8,128)(2,1)}, u32[]{:S(2)}, u32[]{:S(2)}) collective-permute-start(bf16[16,32,1024]{2,1,0:T(8,128)(2,1)S(1)} %constant_dynamic-update-slice_fusion.refs_0_), channel_id=1, source_target_pairs={{0,16},{8,24},{16,0},{24,8},{1,17},{9,25},{17,1},{25,9},{2,18},{10... | collective-permute-start | bytes 3145736 | tf_op jit(solution)/shard_map/ppermute | solution.py:225
  81.2 46.4 %collective-permute-start.9 = (bf16[16,32,1024]{2,1,0:T(8,128)(2,1)S(1)}, bf16[16,32,1024]{2,1,0:T(8,128)(2,1)}, u32[]{:S(2)}, u32[]{:S(2)}) collective-permute-start(bf16[16,32,1024]{2,1,0:T(8,128)(2,1)S(1)} %constant_dynamic-update-slice_fusion.refs_0_), channel_id=1, source_target_pairs={{0,24},{8,16},{16,8},{24,0},{1,25},{9,17},{17,9},{25,1},{2,26},{10... | collective-permute-start | bytes 3145736 | tf_op jit(solution)/shard_map/ppermute | solution.py:225
  127.5 3.0 %collective-permute-start.14 = (bf16[16,32,1024]{2,1,0:T(8,128)(2,1)}, bf16[16,32,1024]{2,1,0:T(8,128)(2,1)}, u32[]{:S(2)}, u32[]{:S(2)}) collective-permute-start(bf16[16,32,1024]{2,1,0:T(8,128)(2,1)} %collective-permute-done.10.refs_0_), channel_id=1, source_target_pairs={{0,1},{1,0},{2,3},{3,2},{4,5},{5,4},{6,7},{7,6},{8,9},{9,8},{10,11... | collective-permute-start | bytes 3145736 | tf_op jit(solution)/shard_map/ppermute | solution.py:222
  130.5 3.0 %collective-permute-start.15 = (bf16[16,32,1024]{2,1,0:T(8,128)(2,1)}, bf16[16,32,1024]{2,1,0:T(8,128)(2,1)}, u32[]{:S(2)}, u32[]{:S(2)}) collective-permute-start(bf16[16,32,1024]{2,1,0:T(8,128)(2,1)} %collective-permute-done.9.refs_2_), channel_id=1, source_target_pairs={{0,1},{1,0},{2,3},{3,2},{4,5},{5,4},{6,7},{7,6},{8,9},{9,8},{10,11... | collective-permute-start | bytes 3145736 | tf_op jit(solution)/shard_map/ppermute | solution.py:222
  130.7 15.5 %copy-start.2 = (f32[17,32,512]{2,1,0:T(8,128)S(1)}, f32[17,32,512]{2,1,0:T(8,128)}, u32[]{:S(2)}) copy-start(f32[17,32,512]{2,1,0:T(8,128)} %contract.2) | copy-start | bytes 3342340
  133.5 24.2 %copy-start.1 = (s32[12,12]{1,0:T(8,128)S(1)}, s32[12,12]{1,0:T(8,128)}, u32[]{:S(2)}) copy-start(s32[12,12]{1,0:T(8,128)} %param.9) | copy-start | bytes 1732
  147.6 6.4 %collective-permute-start.16 = (bf16[128,512]{1,0:T(8,128)(2,1)S(1)}, bf16[128,512]{1,0:T(8,128)(2,1)S(1)}, u32[]{:S(2)}, u32[]{:S(2)}) collective-permute-start(bf16[128,512]{1,0:T(8,128)(2,1)S(1)} %bitcast.61), channel_id=1, source_target_pairs={{0,8},{8,0},{16,24},{24,16},{1,9},{9,1},{17,25},{25,17},{2,10},{10... | collective-permute-start | bytes 393224 | tf_op jit(solution)/shard_map/ppermute | solution.py:225
  148.5 6.8 %collective-permute-start.17 = (bf16[128,512]{1,0:T(8,128)(2,1)S(1)}, bf16[128,512]{1,0:T(8,128)(2,1)S(1)}, u32[]{:S(2)}, u32[]{:S(2)}) collective-permute-start(bf16[128,512]{1,0:T(8,128)(2,1)S(1)} %bitcast.60), channel_id=1, source_target_pairs={{0,16},{8,24},{16,0},{24,8},{1,17},{9,25},{17,1},{25,9},{2,18},{10... | collective-permute-start | bytes 393224 | tf_op jit(solution)/shard_map/ppermute | solution.py:225
  149.7 7.2 %collective-permute-start.18 = (bf16[128,512]{1,0:T(8,128)(2,1)S(1)}, bf16[128,512]{1,0:T(8,128)(2,1)S(1)}, u32[]{:S(2)}, u32[]{:S(2)}) collective-permute-start(bf16[128,512]{1,0:T(8,128)(2,1)S(1)} %bitcast.59), channel_id=1, source_target_pairs={{0,24},{8,16},{16,8},{24,0},{1,25},{9,17},{17,9},{25,1},{2,26},{10... | collective-permute-start | bytes 393224 | tf_op jit(solution)/shard_map/ppermute | solution.py:225
